TPU v7x, 32 devices: a whole 2x2x4 slice. The times are simulated.
32 devices in a mesh: row: 4 (over y, core), col: 8 (over z, x).
Axes of the slice: x: 2, y: 2, z: 4, core: 2. Of those that a mesh axis runs over, the one named last changes fastest.
Arguments:
- phase: float32 [512, 32, 512], P('col', 'row'), may hold values from -6 to 6
- velocity: float32 [3, 512, 32, 512], P(None, 'col', 'row'), may hold values from -12 to 12
Outputs:
- phase_next: float32 [512, 32, 512], P('col', 'row')
- velocity_next: float32 [3, 512, 32, 512], P(None, 'col', 'row')
All inputs are finite; a program needn't handle non-finite values.
Results may differ from a plain program's by a relative error of at most 0.013.
Values may be sent and summed in bfloat16 or wider, within the bound.
A program may use at most 128 MiB of HBM per device.

v0:
```python
import math

import jax
import jax.numpy as jnp
import ml_dtypes
import numpy as np
from jax import lax
from jax.experimental import pallas as pl
from jax.experimental.pallas import tpu as pltpu
from jax.sharding import PartitionSpec as P

NX = 512
NY = 512
KC = 192
KY = 384


time_step = 0.001
epsilon = 0.01
mobility = 1.0
reynolds = 100.0
stabilizer = 2.0


def cos_sin(row_index, col_index, period):
    residue = row_index[:, None] * col_index[None, :] % period
    angles = residue.astype(jnp.float32) * (2.0 * math.pi / period)
    return jnp.stack([jnp.cos(angles), jnp.sin(angles)]).astype(jnp.bfloat16)


def pair_sum(pieces, direction, stack_axis):
    if direction < 0:
        real_part = pieces[0, 0] + pieces[1, 1]
        imag_part = pieces[1, 0] - pieces[0, 1]
    else:
        real_part = pieces[0, 0] - pieces[1, 1]
        imag_part = pieces[0, 1] + pieces[1, 0]
    return jnp.stack([real_part, imag_part], axis=stack_axis)


def times_i(values):
    return jnp.stack([-values[:, 1], values[:, 0]], axis=1)


def phase_terms(phase, velocity, gradient, lap_field):
    advect = velocity[0] * gradient[0] + velocity[1] * gradient[1] + velocity[2] * gradient[2]
    bulk_term = phase * phase * phase - phase
    potential = bulk_term - epsilon * epsilon * lap_field
    return (advect, bulk_term, potential)


def momentum(velocity, vortex, gradient, potential):
    return jnp.stack(
        [
            velocity[1] * vortex[2] - velocity[2] * vortex[1] + potential * gradient[0],
            velocity[2] * vortex[0] - velocity[0] * vortex[2] + potential * gradient[1],
            velocity[0] * vortex[1] - velocity[1] * vortex[0] + potential * gradient[2],
        ]
    )


def plain_device(phase, velocity):
    col_count = lax.axis_size("col")
    row_count = lax.axis_size("row")
    rows_y = phase.shape[0]
    planes = phase.shape[1]
    total_z = planes * row_count
    half_z = 3 * total_z // 8
    modes_z = 2 * half_z
    kx_local = KC // col_count
    ky_local = KY // row_count
    scale_inv = 1.0 / (NX * NY * total_z)
    table_x = cos_sin(jnp.arange(NX, dtype=jnp.int32), jnp.arange(KC, dtype=jnp.int32), NX)
    table_y = cos_sin(jnp.arange(NY, dtype=jnp.int32), jnp.arange(KY, dtype=jnp.int32) - KC, NY)
    table_z = cos_sin(
        jnp.arange(total_z, dtype=jnp.int32), jnp.arange(modes_z, dtype=jnp.int32) - half_z, total_z
    )
    y_forward = table_y.reshape(2, col_count, rows_y, KY)
    y_inverse = table_y.reshape(2, col_count, rows_y, row_count, ky_local)
    z_table = table_z.reshape(2, row_count, planes, modes_z)
    weight = jnp.where(jnp.arange(KC) == 0, 1.0, 2.0).astype(jnp.bfloat16)[:, None, None, None]

    def along_y(incoming):
        field_count = incoming.shape[1]
        shaped = incoming.reshape(incoming.shape[0], field_count, col_count, 2, rows_y, planes)
        pieces = jnp.einsum(
            "afcpyz,tcyb->ptafbz", shaped, y_forward, preferred_element_type=jnp.float32
        )
        joined = pair_sum(pieces, -1, 2).astype(jnp.bfloat16)
        return joined.reshape(incoming.shape[0], field_count, 2, KY * planes)

    def along_z(incoming):
        field_count = incoming.shape[1]
        shaped = incoming.reshape(incoming.shape[0], field_count, 2, row_count, ky_local, planes)
        pieces = jnp.einsum(
            "afprbz,trzm->ptafbm", shaped, z_table, preferred_element_type=jnp.float32
        )
        joined = pair_sum(pieces, -1, 2) * scale_inv
        return joined.reshape(incoming.shape[0], field_count, 2, ky_local * modes_z)

    def back_y(incoming):
        field_count = incoming.shape[1]
        shaped = incoming.reshape(incoming.shape[0], field_count, 2, row_count, planes, ky_local)
        pieces = jnp.einsum(
            "afprzb,tcyrb->ptafcyz", shaped, y_inverse, preferred_element_type=jnp.float32
        )
        joined = pair_sum(pieces, 1, 3).astype(jnp.bfloat16)
        return joined.reshape(incoming.shape[0], field_count, col_count * 2 * rows_y * planes)

    def back_x(incoming):
        field_count = incoming.shape[1]
        shaped = incoming.reshape(KC, field_count, 2, rows_y, planes)
        scaled = jnp.stack([shaped[:, :, 0] * weight, -(shaped[:, :, 1] * weight)], axis=2)
        return jnp.einsum("afpyz,pxa->fyzx", scaled, table_x, preferred_element_type=jnp.float32)

    def forward(fields):
        field_count = fields.shape[0]
        pieces = jnp.einsum(
            "fyzx,txa->tafyz",
            fields.astype(jnp.bfloat16),
            table_x,
            preferred_element_type=jnp.float32,
        )
        x_lines = jnp.stack([pieces[0], -pieces[1]], axis=2).astype(jnp.bfloat16)
        x_lines = x_lines.reshape(KC, field_count, 2 * rows_y * planes)
        spread = along_y(lax.all_to_all(x_lines, "col", split_axis=0, concat_axis=2, tiled=True))
        return along_z(lax.all_to_all(spread, "row", split_axis=3, concat_axis=3, tiled=True))

    def inverse(spectra):
        field_count = spectra.shape[1]
        shaped = spectra.astype(jnp.bfloat16).reshape(kx_local, field_count, 2, ky_local, modes_z)
        pieces = jnp.einsum(
            "afpbm,trzm->ptafrzb", shaped, z_table, preferred_element_type=jnp.float32
        )
        z_planes = (
            pair_sum(pieces, 1, 2)
            .astype(jnp.bfloat16)
            .reshape(kx_local, field_count, 2, total_z * ky_local)
        )
        spread = back_y(lax.all_to_all(z_planes, "row", split_axis=3, concat_axis=3, tiled=True))
        return back_x(lax.all_to_all(spread, "col", split_axis=2, concat_axis=0, tiled=True))

    spectra = forward(jnp.concatenate([phase[None], velocity], axis=0))
    wave_x = (lax.axis_index("col") * kx_local + jnp.arange(kx_local, dtype=jnp.int32)).astype(
        jnp.float32
    )[:, None, None]
    modes_y = lax.axis_index("row") * ky_local + jnp.arange(ky_local, dtype=jnp.int32) - KC
    wave_y = jnp.broadcast_to(modes_y.astype(jnp.float32)[:, None], (ky_local, modes_z)).reshape(-1)
    z_values = (jnp.arange(modes_z, dtype=jnp.int32) - half_z).astype(jnp.float32) * (NX / total_z)
    wave_z = jnp.broadcast_to(z_values[None, :], (ky_local, modes_z)).reshape(-1)
    squared = wave_x * wave_x + wave_y * wave_y + wave_z * wave_z
    coeff_phase = spectra[:, 0]
    coeff_u = spectra[:, 1]
    coeff_v = spectra[:, 2]
    coeff_w = spectra[:, 3]
    gradients = [
        times_i(wave_x * coeff_phase),
        times_i(wave_y * coeff_phase),
        times_i(wave_z * coeff_phase),
    ]
    laplace = -squared * coeff_phase
    vortex_hat = [
        times_i(wave_y * coeff_w - wave_z * coeff_v),
        times_i(wave_z * coeff_u - wave_x * coeff_w),
        times_i(wave_x * coeff_v - wave_y * coeff_u),
    ]
    leading = inverse(jnp.stack(gradients + [laplace], axis=1))
    advect, bulk_term, potential = phase_terms(phase, velocity, leading[0:3], leading[3])
    phase_side = forward(jnp.stack([advect, bulk_term]))
    vortex = inverse(jnp.stack(vortex_hat, axis=1))
    flow_side = forward(momentum(velocity, vortex, leading[0:3], potential))
    nonlinear = jnp.concatenate([phase_side, flow_side], axis=1)
    mean_mode = (wave_x == 0) & (wave_y == 0) & (wave_z == 0)
    advect_hat = jnp.where(mean_mode, 0.0, nonlinear[:, 0])
    bulk_hat = nonlinear[:, 1]
    stable_part = 1.0 / time_step + mobility * stabilizer * squared
    new_phase = (stable_part * coeff_phase - advect_hat - mobility * squared * bulk_hat) / (
        stable_part + mobility * epsilon * epsilon * squared * squared
    )
    viscous = 1.0 / time_step + squared / reynolds
    unprojected = [
        (spectra[:, 1 + j] / time_step + nonlinear[:, 2 + j]) / viscous for j in range(3)
    ]
    normal_part = (
        wave_x * unprojected[0] + wave_y * unprojected[1] + wave_z * unprojected[2]
    ) / jnp.maximum(squared, 1.0)
    waves = [wave_x, wave_y, wave_z]
    new_flow = [unprojected[j] - waves[j] * normal_part for j in range(3)]
    result = inverse(jnp.stack([new_phase] + new_flow, axis=1))
    return (result[0], result[1:4])


def tables(cols, rows, rows_y, planes):
    total_z = planes * rows
    half_z = 3 * total_z // 8
    modes_z = 2 * half_z
    kx_local = KC // cols

    def pair(first, second, period):
        residue = first[:, None] * second[None, :] % period
        angles = residue.astype(np.float32) * np.float32(2.0 * math.pi / period)
        return [np.cos(angles).astype(ml_dtypes.bfloat16), np.sin(angles).astype(ml_dtypes.bfloat16)]

    cos_x, sin_x = pair(np.arange(KC), np.arange(NX), NX)
    cos_y, sin_y = pair(np.arange(NY), np.arange(KY) - KC, NY)
    cos_z, sin_z = pair(np.arange(total_z), np.arange(modes_z) - half_z, total_z)
    x_forward = np.stack([cos_x, -sin_x]).reshape(2, cols, kx_local, NX)
    x_forward = x_forward.transpose(1, 0, 2, 3).reshape(2 * KC, NX)
    weight = np.where(np.arange(KC) == 0, 1.0, 2.0).astype(ml_dtypes.bfloat16)[:, None]
    x_inverse = np.stack([cos_x * weight, -(sin_x * weight)]).reshape(2, cols, kx_local, NX)
    x_inverse = x_inverse.transpose(1, 0, 2, 3).reshape(2 * KC, NX)
    y_forward = np.concatenate([cos_y, sin_y], axis=1)
    y_inverse = np.concatenate([cos_y.T, sin_y.T], axis=1)
    cz, sz = (t.reshape(rows, planes, modes_z) for t in (cos_z, sin_z))
    z_forward = np.stack([np.stack([cz, sz], 1), np.stack([-sz, cz], 1)])
    z_forward = z_forward.transpose(0, 4, 1, 2, 3).reshape(2 * modes_z, 2 * total_z)
    z_inverse = np.stack([np.stack([cz, -sz], 2), np.stack([sz, cz], 2)], 1)
    z_inverse = z_inverse.reshape(2 * total_z, 2 * modes_z)
    return [jnp.asarray(t.astype(ml_dtypes.bfloat16)) for t in (x_forward, x_inverse, y_forward, y_inverse, z_forward, z_inverse)]


def dot(first, second, dims=((1,), (0,))):
    return lax.dot_general(first, second, (dims, ((), ())), preferred_element_type=jnp.float32)


def whole(array):
    return pl.BlockSpec(array.shape, lambda *_: (0,) * array.ndim)


def call(body, grid, in_specs, out_specs, out_shape, flops, moved, scratch=()):
    return pl.pallas_call(
        body,
        grid=grid,
        in_specs=in_specs,
        out_specs=out_specs,
        out_shape=out_shape,
        scratch_shapes=list(scratch),
        compiler_params=pltpu.CompilerParams(vmem_limit_bytes=40 * 1024 * 1024),
        cost_estimate=pl.CostEstimate(flops=flops, bytes_accessed=moved, transcendentals=0),
    )


COST = 400_000_000


def fast_device(sizes, phase, velocity):
    cols, rows, rows_y, planes = sizes
    total_z = planes * rows
    half_z = 3 * total_z // 8
    modes_z = 2 * half_z
    kx_local = KC // cols
    a_local = kx_local // rows
    lanes = a_local * KY
    points = rows_y * planes
    scale_inv = 1.0 / (NX * NY * total_z)
    tx_f, tx_i, ty_f, ty_i, tz_f, tz_i = tables(cols, rows, rows_y, planes)
    f32, bf16 = jnp.float32, jnp.bfloat16

    def exchange(axis, size, src, dst, send, recv):
        me = lax.axis_index(axis)

        def copy(f, d):
            peer = lax.rem(me + d, size)
            return pltpu.make_async_remote_copy(
                src_ref=src.at[f, peer],
                dst_ref=dst.at[f, me],
                send_sem=send.at[f, d - 1],
                recv_sem=recv.at[f, d - 1],
                device_id={axis: peer},
                device_id_type=pl.DeviceIdType.MESH,
            )

        def start(f):
            for d in range(1, size):
                copy(f, d).start()

        def wait_recv(f):
            for d in range(1, size):
                copy(f, d).wait_recv()

        def wait_send(f):
            for d in range(1, size):
                copy(f, d).wait_send()

        def keep(f):
            dst[f, me] = src[f, me]

        return start, wait_recv, wait_send, keep

    def greet():
        barrier = pltpu.get_barrier_semaphore()
        for axis, size in (("col", cols), ("row", rows)):
            for d in range(1, size):
                peer = lax.rem(lax.axis_index(axis) + d, size)
                pl.semaphore_signal(
                    barrier, inc=1, device_id={axis: peer}, device_id_type=pl.DeviceIdType.MESH
                )
        pl.semaphore_wait(barrier, cols + rows - 2)

    def two_exchanges(operands, count, first, second, prepare, compute, unfold, ident):
        (axis1, size1, shape1), (axis2, size2, shape2) = first, second
        ins = len(operands)

        def body(*refs):
            in_refs, out_ref = refs[:ins], refs[ins]
            got, made, send1, recv1, send2, recv2 = refs[ins + 1 : ins + 7]
            more = list(refs[ins + 7 :])
            source = more.pop(0) if prepare else in_refs[0]
            landed = more.pop(0) if unfold else out_ref
            start1, recv_1, sent1, keep1 = exchange(axis1, size1, source, got, send1, recv1)
            start2, recv_2, sent2, keep2 = exchange(axis2, size2, made, landed, send2, recv2)
            if prepare:
                prepare(0, in_refs, source)
            greet()
            start1(0)

            def begin(f, carry):
                if prepare:
                    prepare(f, in_refs, source)
                start1(f)
                return carry

            lax.fori_loop(1, count, begin, 0)

            def step(f, carry):
                keep1(f)
                recv_1(f)
                compute(f, got, in_refs, made)
                start2(f)
                keep2(f)
                return carry

            lax.fori_loop(0, count, step, 0)

            def finish(f, carry):
                recv_2(f)
                if unfold:
                    unfold(f, landed, in_refs, out_ref)
                sent1(f)
                sent2(f)
                return carry

            lax.fori_loop(0, count, finish, 0)

        sems = pltpu.SemaphoreType.DMA
        scratch = [
            pltpu.VMEM((count,) + shape1, bf16),
            pltpu.VMEM((count,) + shape2, bf16),
            sems((count, size1 - 1)),
            sems((count, size1 - 1)),
            sems((count, size2 - 1)),
            sems((count, size2 - 1)),
        ]
        if prepare:
            scratch.append(pltpu.VMEM((count,) + shape1, bf16))
        if unfold:
            scratch.append(pltpu.VMEM((count,) + shape2, bf16))
            out_shape = jax.ShapeDtypeStruct((count, rows_y, planes, NX), f32)
        else:
            out_shape = jax.ShapeDtypeStruct((count,) + shape2, bf16)
        return pl.pallas_call(
            body,
            in_specs=[pl.BlockSpec(memory_space=pltpu.VMEM)] * ins,
            out_specs=pl.BlockSpec(memory_space=pltpu.VMEM),
            out_shape=out_shape,
            scratch_shapes=scratch,
            compiler_params=pltpu.CompilerParams(
                collective_id=ident, has_side_effects=True, vmem_limit_bytes=40 * 1024 * 1024
            ),
            cost_estimate=pl.CostEstimate(
                flops=COST * count, bytes_accessed=1 << 20, transcendentals=0
            ),
        )(*operands)

    col_side = ("col", cols, (cols, 2 * kx_local, points))
    row_side = ("row", rows, (rows, 2 * planes, lanes))

    def y_forward(f, in_ref, in_refs, out_ref):
        table_ref = in_refs[-1]
        lhs = jnp.concatenate(
            [
                jnp.concatenate(
                    [in_ref[f, c, :, z * rows_y : (z + 1) * rows_y] for c in range(cols)], axis=1
                )
                for z in range(planes)
            ],
            axis=0,
        )
        made = dot(lhs, table_ref[...]).reshape(planes, 2 * kx_local, 2 * KY)
        first, second = made[:, :kx_local], made[:, kx_local:]
        real = jnp.swapaxes(first[:, :, :KY] + second[:, :, KY:], 0, 1)
        imag = jnp.swapaxes(second[:, :, :KY] - first[:, :, KY:], 0, 1)
        both = jnp.concatenate([real, imag], axis=1).astype(bf16)
        for a in range(kx_local):
            r, k = a // a_local, a % a_local
            out_ref[f, r, :, k * KY : (k + 1) * KY] = both[a]

    def y_inverse(f, in_ref, in_refs, out_ref):
        table_ref = in_refs[-1]
        lhs = jnp.concatenate(
            [in_ref[f, r, :, k * KY : (k + 1) * KY] for r in range(rows) for k in range(a_local)],
            axis=0,
        )
        made = dot(lhs, table_ref[...]).reshape(kx_local, 2 * planes, 2 * NY)
        first, second = made[:, :planes], made[:, planes:]
        real = jnp.swapaxes(first[:, :, :NY] - second[:, :, NY:], 0, 1)
        imag = jnp.swapaxes(first[:, :, NY:] + second[:, :, :NY], 0, 1)
        both = jnp.concatenate([real, imag], axis=1).astype(bf16)
        for c in range(cols):
            out_ref[f, c] = jnp.concatenate(
                [both[z, :, c * rows_y : (c + 1) * rows_y] for z in range(planes)], axis=1
            )

    def x_lines(field, table_ref):
        lines = jnp.swapaxes(field, 0, 1).reshape(points, NX).astype(bf16)
        made = dot(table_ref[...], lines, ((1,), (1,))).astype(bf16)
        return made.reshape(cols, 2 * kx_local, points)

    def x_field(lines, table_ref):
        made = dot(lines.reshape(2 * KC, points), table_ref[...], ((0,), (0,)))
        return jnp.swapaxes(made.reshape(planes, rows_y, NX), 0, 1)

    def first_to_spectral():
        def prepare(f, in_refs, source):
            phase_ref, flow_ref, table_ref, _ = in_refs
            if isinstance(f, int):
                source[f] = x_lines(phase_ref[...], table_ref)
                return

            @pl.when(f < 4)
            def _():
                source[f] = x_lines(flow_ref[jnp.minimum(f - 1, 2)], table_ref)

            @pl.when(f == 4)
            def _():
                c = phase_ref[...]
                source[f] = x_lines(c * c * c - c, table_ref)

        operands = (phase, velocity, tx_f, ty_f)
        return two_exchanges(operands, 5, col_side, row_side, prepare, y_forward, None, 0)

    def products_to_spectral(products):
        def prepare(f, in_refs, source):
            source[f] = x_lines(in_refs[0][f], in_refs[1])

        operands = (products, tx_f, ty_f)
        return two_exchanges(operands, 4, col_side, row_side, prepare, y_forward, None, 2)

    def derived_to_physical(derived):
        def unfold(f, landed, in_refs, out_ref):
            out_ref[f] = x_field(landed[f], in_refs[1])

        operands = (derived, tx_i, ty_i)
        return two_exchanges(operands, 7, row_side, col_side, None, y_inverse, unfold, 1)

    def solved_to_lines(solved):
        return two_exchanges((solved, ty_i), 4, row_side, col_side, None, y_inverse, None, 3)

    def x_inverse(incoming, begin, count):
        def body(in_ref, table_ref, out_ref):
            out_ref[0] = x_field(in_ref[0], table_ref)

        return call(
            body,
            (count,),
            [
                pl.BlockSpec((1, cols, 2 * kx_local, points), lambda i: (i + begin, 0, 0, 0)),
                whole(tx_i),
            ],
            pl.BlockSpec((1, rows_y, planes, NX), lambda i: (i, 0, 0, 0)),
            jax.ShapeDtypeStruct((count, rows_y, planes, NX), f32),
            COST * count,
            1 << 20,
        )(incoming, tx_i)

    cut = KY
    steps = lanes // cut
    first_a = lax.axis_index("col") * kx_local + lax.axis_index("row") * a_local
    wave_x = first_a.astype(f32) + jnp.repeat(jnp.arange(a_local, dtype=f32), KY)
    wave_y = jnp.tile(jnp.arange(KY, dtype=f32) - KC, a_local)
    wave_xy = jnp.stack([wave_x, wave_y])

    def coefficient(in_ref, f, table_ref):
        stacked = jnp.concatenate([in_ref[f, r] for r in range(rows)], axis=0)
        return dot(table_ref[...], stacked) * scale_inv

    def emit(out_ref, f, real, imag, table_ref):
        both = jnp.concatenate([real, imag], axis=0).astype(bf16)
        made = dot(table_ref[...], both).astype(bf16)
        for r in range(rows):
            out_ref[f, r] = made[r * 2 * planes : (r + 1) * 2 * planes]

    def waves(wave_ref):
        wx, wy = wave_ref[0:1, :], wave_ref[1:2, :]
        m = lax.broadcasted_iota(jnp.int32, (modes_z, cut), 0) - half_z
        wz = m.astype(f32) * (NX / total_z)
        return wx, wy, wz, wx * wx + wy * wy + wz * wz

    def lines_spec(count):
        return pl.BlockSpec((count, rows, 2 * planes, cut), lambda i: (0, 0, 0, i))

    def coeff_spec(count):
        return pl.BlockSpec((count, 2 * modes_z, cut), lambda i: (0, 0, i))

    def lines_shape(count):
        return jax.ShapeDtypeStruct((count, rows, 2 * planes, lanes), bf16)

    def coeff_shape(count):
        return jax.ShapeDtypeStruct((count, 2 * modes_z, lanes), f32)

    wave_spec = pl.BlockSpec((2, cut), lambda i: (0, i))

    def derive(in_ref, wave_ref, f_ref, i_ref, coeff_ref, out_ref):
        wx, wy, wz, k2 = waves(wave_ref)
        cs = [coefficient(in_ref, j, f_ref) for j in range(5)]
        for j in range(5):
            coeff_ref[j] = cs[j]
        re, im = [c[:modes_z] for c in cs], [c[modes_z:] for c in cs]
        emit(out_ref, 0, -(wx * im[0]), wx * re[0], i_ref)
        emit(out_ref, 1, -(wy * im[0]), wy * re[0], i_ref)
        emit(out_ref, 2, -(wz * im[0]), wz * re[0], i_ref)
        emit(out_ref, 3, -k2 * re[0], -k2 * im[0], i_ref)
        w = [wx, wy, wz]
        for j in range(3):
            p, q = (j + 1) % 3, (j + 2) % 3
            real = -(w[p] * im[1 + q] - w[q] * im[1 + p])
            emit(out_ref, 4 + j, real, w[p] * re[1 + q] - w[q] * re[1 + p], i_ref)

    def solve(in_ref, old_ref, wave_ref, f_ref, i_ref, out_ref):
        wx, wy, wz, k2 = waves(wave_ref)
        mean_mode = (wx == 0) & (wy == 0) & (wz == 0)
        stable = 1.0 / time_step + mobility * stabilizer * k2
        below = stable + mobility * epsilon * epsilon * k2 * k2
        viscous = 1.0 / time_step + k2 / reynolds
        largest = jnp.maximum(k2, 1.0)
        w = [wx, wy, wz]
        added = [coefficient(in_ref, j, f_ref) for j in range(4)]
        made = [[], [], [], []]
        for p in range(2):
            at = slice(p * modes_z, (p + 1) * modes_z)
            kept = jnp.where(mean_mode, 0.0, added[0][at])
            made[0].append((stable * old_ref[0, at] - kept - mobility * k2 * old_ref[4, at]) / below)
            free = [(old_ref[1 + j, at] / time_step + added[1 + j][at]) / viscous for j in range(3)]
            normal = (wx * free[0] + wy * free[1] + wz * free[2]) / largest
            for j in range(3):
                made[1 + j].append(free[j] - w[j] * normal)
        for j in range(4):
            emit(out_ref, j, made[j][0], made[j][1], i_ref)

    tail = [wave_spec, whole(tz_f), whole(tz_i)]
    last = (wave_xy, tz_f, tz_i)
    first_lines = first_to_spectral()
    coeffs, derived = call(
        derive, (steps,), [lines_spec(5)] + tail,
        [coeff_spec(5), lines_spec(7)], [coeff_shape(5), lines_shape(7)], COST, 1 << 20,
    )(first_lines, *last)
    fields = derived_to_physical(derived)
    gradient, vortex = fields[0:3], fields[4:7]
    advect, _, potential = phase_terms(phase, velocity, gradient, fields[3])
    forcing = momentum(velocity, vortex, gradient, potential)
    products = jnp.concatenate([advect[None], forcing], axis=0)
    product_lines = products_to_spectral(products)
    solved = call(
        solve, (steps,), [lines_spec(4), coeff_spec(5)] + tail,
        lines_spec(4), lines_shape(4), COST, 1 << 20,
    )(product_lines, coeffs, *last)
    solved_lines = solved_to_lines(solved)
    return (x_inverse(solved_lines, 0, 1)[0], x_inverse(solved_lines, 1, 3))


def solution(mesh):
    cols, rows = mesh.shape["col"], mesh.shape["row"]

    def on_device(phase, velocity):
        rows_y, planes = phase.shape[0], phase.shape[1]
        kx_local = KC // cols
        aligned = planes % 8 == 0 and kx_local % (8 * rows // math.gcd(8, rows)) == 0
        if aligned and (rows_y * planes) % 128 == 0:
            return fast_device((cols, rows, rows_y, planes), phase, velocity)
        return plain_device(phase, velocity)

    return jax.shard_map(
        on_device,
        mesh=mesh,
        in_specs=(P("col", "row", None), P(None, "col", "row", None)),
        out_specs=(P("col", "row", None), P(None, "col", "row", None)),
        check_vma=False,
    )
```

profile of v0, /device:TPU:0, one launch (start us, length us, event | category | flops | bytes accessed | tf_op | source)
XLA Modules:
  0.0 230.9 jit_solution(3770467388052459865)
XLA Ops:
  0.6 0.0 copy-start.9
  0.6 0.0 copy-start.10
  0.8 0.0 copy-start
  0.8 1.9 copy-done
  2.7 1.2 copy-done.3
  3.9 1.1 copy-done.5
  5.0 1.0 copy-done.7
  6.0 52.7 %shard_map.95.in_ref = bf16[5,4,16,2304]{3,2,1,0:T(8,128)(2,1)S(1)} custom-call(f32[64,8,512]{2,1,0:T(8,128)S(1)} %copy-done.3, f32[3,64,8,512]{3,2,1,0:T(8,128)S(1)} %copy-done, bf16[384,512]{1,0:T(8,128)(2,1)S(1)} %copy-done.7, bf16[512,768]{1,0:T(8,128)(2,1)S(1)} %copy-done.5), custom_call_target="tpu_custom_call" | custom-call | flops 2000000000 | bytes 1048576 | tf_op jit(solution)/shard_map/pallas_call | solution.py:361
  58.8 0.0 copy-done.9
  58.8 2.8 %shard_map.96 = (f32[5,48,2304]{2,1,0:T(8,128)S(1)}, bf16[7,4,16,2304]{3,2,1,0:T(8,128)(2,1)S(1)}) custom-call(bf16[5,4,16,2304]{3,2,1,0:T(8,128)(2,1)S(1)} %shard_map.95.in_ref, f32[2,2304]{1,0:T(2,128)S(1)} %pad_maximum_fusion.1.wave_ref, bf16[48,64]{1,0:T(8,128)(2,1)S(1)} %copy-done.10, bf16[64,48]{1,0:T(8,128)(2,1)S(1)} %copy-done.9), custom_call_target="tpu_custom_call" | custom-call | flops 400000000 | bytes 1048576 | tf_op jit(solution)/shard_map/pallas_call | solution.py:553
  61.7 0.0 copy-start.1
  61.7 69.1 %shard_map.97 = f32[7,64,8,512]{3,2,1,0:T(8,128)S(1)} custom-call(bf16[7,4,16,2304]{3,2,1,0:T(8,128)(2,1)S(1)} %get-tuple-element.4.refs_0_, bf16[384,512]{1,0:T(8,128)(2,1)S(1)} %copy-done.2, bf16[384,1024]{1,0:T(8,128)(2,1)S(1)} %copy-done.4), custom_call_target="tpu_custom_call" | custom-call | flops 2800000000 | bytes 1048576 | tf_op jit(solution)/shard_map/pallas_call | solution.py:361
  130.8 0.8 multiply_add_fusion
  131.5 1.5 fusion.6
  133.0 0.0 copy-start.6
  133.0 0.0 copy-start.8
  133.0 0.5 pad_maximum_fusion.refs_0_
  133.6 0.6 copy-done.6
  134.1 0.1 copy-done.8
  134.2 45.3 %shard_map.98.in_ref = bf16[4,4,16,2304]{3,2,1,0:T(8,128)(2,1)S(1)} custom-call(f32[4,64,8,512]{3,2,1,0:T(8,128)S(1)} %pad_maximum_fusion.refs_0_, bf16[384,512]{1,0:T(8,128)(2,1)S(1)} %copy-done.8, bf16[512,768]{1,0:T(8,128)(2,1)S(1)} %copy-done.6), custom_call_target="tpu_custom_call" | custom-call | flops 1600000000 | bytes 1048576 | tf_op jit(solution)/shard_map/pallas_call | solution.py:361
  179.5 2.7 %shard_map.99.refs_0_ = bf16[4,4,16,2304]{3,2,1,0:T(8,128)(2,1)S(1)} custom-call(bf16[4,4,16,2304]{3,2,1,0:T(8,128)(2,1)S(1)} %shard_map.98.in_ref, f32[5,48,2304]{2,1,0:T(8,128)S(1)} %get-tuple-element.5.old_ref, f32[2,2304]{1,0:T(2,128)S(1)} %pad_maximum_fusion.1.wave_ref, bf16[48,64]{1,0:T(8,128)(2,1)S(1)} %copy-done.10, bf16[64,48]{1,0:T(8,128)(2,1)S(1)} %copy-done.9), custom_call_target="tpu_custom_call" | custom-call | flops 400000000 | bytes 1048576 | tf_op jit(solution)/shard_map/pallas_call | solution.py:563
  182.3 44.0 %shard_map.100.in_ref = bf16[4,8,48,512]{3,2,1,0:T(8,128)(2,1)S(1)} custom-call(bf16[4,4,16,2304]{3,2,1,0:T(8,128)(2,1)S(1)} %shard_map.99.refs_0_, bf16[384,1024]{1,0:T(8,128)(2,1)S(1)} %copy-done.4), custom_call_target="tpu_custom_call" | custom-call | flops 1600000000 | bytes 1048576 | tf_op jit(solution)/shard_map/pallas_call | solution.py:361
  226.3 1.5 shard_map.101
  227.8 3.1 %shard_map.102 = f32[3,64,8,512]{3,2,1,0:T(8,128)} custom-call(bf16[4,8,48,512]{3,2,1,0:T(8,128)(2,1)S(1)} %shard_map.100.in_ref, bf16[384,512]{1,0:T(8,128)(2,1)S(1)} %copy-done.2), custom_call_target="tpu_custom_call" | custom-call | flops 1200000000 | bytes 1048576 | tf_op jit(solution)/shard_map/pallas_call | solution.py:463
  (15 shorter events, 0.1 us)
Async XLA Ops:
  0.6 58.2 %copy-start.9 = (bf16[64,48]{1,0:T(8,128)(2,1)S(1)}, bf16[64,48]{1,0:T(8,128)(2,1)}, u32[]{:S(2)}) copy-start(bf16[64,48]{1,0:T(8,128)(2,1)} %constant.34.clone.i_ref) | copy-start | bytes 18436
  0.6 58.1 %copy-start.10 = (bf16[48,64]{1,0:T(8,128)(2,1)S(1)}, bf16[48,64]{1,0:T(8,128)(2,1)}, u32[]{:S(2)}) copy-start(bf16[48,64]{1,0:T(8,128)(2,1)} %constant.33.clone.f_ref) | copy-start | bytes 18436
  0.8 1.9 copy-start
  2.7 1.2 copy-start.3
  3.9 1.1 copy-start.5
  5.0 1.0 copy-start.7
  6.0 55.6 %copy-start.2 = (bf16[384,512]{1,0:T(8,128)(2,1)S(1)}, bf16[384,512]{1,0:T(8,128)(2,1)}, u32[]{:S(2)}) copy-start(bf16[384,512]{1,0:T(8,128)(2,1)} %constant.30.clone.refs_1_.table_ref) | copy-start | bytes 1179652
  6.0 55.6 %copy-start.4 = (bf16[384,1024]{1,0:T(8,128)(2,1)S(1)}, bf16[384,1024]{1,0:T(8,128)(2,1)}, u32[]{:S(2)}) copy-start(bf16[384,1024]{1,0:T(8,128)(2,1)} %constant.32.clone.refs_2_.refs_1_) | copy-start | bytes 2359300
  61.7 69.1 %copy-start.1 = (f32[3,64,8,512]{3,2,1,0:T(8,128)S(1)}, f32[3,64,8,512]{3,2,1,0:T(8,128)}, u32[]{:S(2)}) copy-start(f32[3,64,8,512]{3,2,1,0:T(8,128)} %refs_1_.4) | copy-start | bytes 9437188
  133.0 1.1 copy-start.6
  133.0 1.2 copy-start.8
where the time goes:
time: 232 us; the launch traced here: 231 us
  Pallas kernels  221 us (95%)
  local copies, waits for them, and re-layouts  5.96 us (3%)
  other arithmetic  2.8 us (1%)
    pallas_call x4, Pallas kernels, two_exchanges(): pl.pallas_call(body, in_specs=[pl.BlockSpec(memory_space=pltpu.VMEM)] * i...  211 us
    unnamed x25, local copies, waits for them, and re-layouts  5.96 us

commit v1 on v0

v1 whole, which is shorter than its diff:
```python
import math

import jax
import jax.numpy as jnp
import ml_dtypes
import numpy as np
from jax import lax
from jax.experimental import pallas as pl
from jax.experimental.pallas import tpu as pltpu
from jax.sharding import PartitionSpec as P

NX = 512
NY = 512
KC = 192
KY = 384


time_step = 0.001
epsilon = 0.01
mobility = 1.0
reynolds = 100.0
stabilizer = 2.0


def cos_sin(row_index, col_index, period):
    residue = row_index[:, None] * col_index[None, :] % period
    angles = residue.astype(jnp.float32) * (2.0 * math.pi / period)
    return jnp.stack([jnp.cos(angles), jnp.sin(angles)]).astype(jnp.bfloat16)


def pair_sum(pieces, direction, stack_axis):
    if direction < 0:
        real_part = pieces[0, 0] + pieces[1, 1]
        imag_part = pieces[1, 0] - pieces[0, 1]
    else:
        real_part = pieces[0, 0] - pieces[1, 1]
        imag_part = pieces[0, 1] + pieces[1, 0]
    return jnp.stack([real_part, imag_part], axis=stack_axis)


def times_i(values):
    return jnp.stack([-values[:, 1], values[:, 0]], axis=1)


def phase_terms(phase, velocity, gradient, lap_field):
    advect = velocity[0] * gradient[0] + velocity[1] * gradient[1] + velocity[2] * gradient[2]
    bulk_term = phase * phase * phase - phase
    potential = bulk_term - epsilon * epsilon * lap_field
    return (advect, bulk_term, potential)


def momentum(velocity, vortex, gradient, potential):
    return jnp.stack(
        [
            velocity[1] * vortex[2] - velocity[2] * vortex[1] + potential * gradient[0],
            velocity[2] * vortex[0] - velocity[0] * vortex[2] + potential * gradient[1],
            velocity[0] * vortex[1] - velocity[1] * vortex[0] + potential * gradient[2],
        ]
    )


def plain_device(phase, velocity):
    col_count = lax.axis_size("col")
    row_count = lax.axis_size("row")
    rows_y = phase.shape[0]
    planes = phase.shape[1]
    total_z = planes * row_count
    half_z = 3 * total_z // 8
    modes_z = 2 * half_z
    kx_local = KC // col_count
    ky_local = KY // row_count
    scale_inv = 1.0 / (NX * NY * total_z)
    table_x = cos_sin(jnp.arange(NX, dtype=jnp.int32), jnp.arange(KC, dtype=jnp.int32), NX)
    table_y = cos_sin(jnp.arange(NY, dtype=jnp.int32), jnp.arange(KY, dtype=jnp.int32) - KC, NY)
    table_z = cos_sin(
        jnp.arange(total_z, dtype=jnp.int32), jnp.arange(modes_z, dtype=jnp.int32) - half_z, total_z
    )
    y_forward = table_y.reshape(2, col_count, rows_y, KY)
    y_inverse = table_y.reshape(2, col_count, rows_y, row_count, ky_local)
    z_table = table_z.reshape(2, row_count, planes, modes_z)
    weight = jnp.where(jnp.arange(KC) == 0, 1.0, 2.0).astype(jnp.bfloat16)[:, None, None, None]

    def along_y(incoming):
        field_count = incoming.shape[1]
        shaped = incoming.reshape(incoming.shape[0], field_count, col_count, 2, rows_y, planes)
        pieces = jnp.einsum(
            "afcpyz,tcyb->ptafbz", shaped, y_forward, preferred_element_type=jnp.float32
        )
        joined = pair_sum(pieces, -1, 2).astype(jnp.bfloat16)
        return joined.reshape(incoming.shape[0], field_count, 2, KY * planes)

    def along_z(incoming):
        field_count = incoming.shape[1]
        shaped = incoming.reshape(incoming.shape[0], field_count, 2, row_count, ky_local, planes)
        pieces = jnp.einsum(
            "afprbz,trzm->ptafbm", shaped, z_table, preferred_element_type=jnp.float32
        )
        joined = pair_sum(pieces, -1, 2) * scale_inv
        return joined.reshape(incoming.shape[0], field_count, 2, ky_local * modes_z)

    def back_y(incoming):
        field_count = incoming.shape[1]
        shaped = incoming.reshape(incoming.shape[0], field_count, 2, row_count, planes, ky_local)
        pieces = jnp.einsum(
            "afprzb,tcyrb->ptafcyz", shaped, y_inverse, preferred_element_type=jnp.float32
        )
        joined = pair_sum(pieces, 1, 3).astype(jnp.bfloat16)
        return joined.reshape(incoming.shape[0], field_count, col_count * 2 * rows_y * planes)

    def back_x(incoming):
        field_count = incoming.shape[1]
        shaped = incoming.reshape(KC, field_count, 2, rows_y, planes)
        scaled = jnp.stack([shaped[:, :, 0] * weight, -(shaped[:, :, 1] * weight)], axis=2)
        return jnp.einsum("afpyz,pxa->fyzx", scaled, table_x, preferred_element_type=jnp.float32)

    def forward(fields):
        field_count = fields.shape[0]
        pieces = jnp.einsum(
            "fyzx,txa->tafyz",
            fields.astype(jnp.bfloat16),
            table_x,
            preferred_element_type=jnp.float32,
        )
        x_lines = jnp.stack([pieces[0], -pieces[1]], axis=2).astype(jnp.bfloat16)
        x_lines = x_lines.reshape(KC, field_count, 2 * rows_y * planes)
        spread = along_y(lax.all_to_all(x_lines, "col", split_axis=0, concat_axis=2, tiled=True))
        return along_z(lax.all_to_all(spread, "row", split_axis=3, concat_axis=3, tiled=True))

    def inverse(spectra):
        field_count = spectra.shape[1]
        shaped = spectra.astype(jnp.bfloat16).reshape(kx_local, field_count, 2, ky_local, modes_z)
        pieces = jnp.einsum(
            "afpbm,trzm->ptafrzb", shaped, z_table, preferred_element_type=jnp.float32
        )
        z_planes = (
            pair_sum(pieces, 1, 2)
            .astype(jnp.bfloat16)
            .reshape(kx_local, field_count, 2, total_z * ky_local)
        )
        spread = back_y(lax.all_to_all(z_planes, "row", split_axis=3, concat_axis=3, tiled=True))
        return back_x(lax.all_to_all(spread, "col", split_axis=2, concat_axis=0, tiled=True))

    spectra = forward(jnp.concatenate([phase[None], velocity], axis=0))
    wave_x = (lax.axis_index("col") * kx_local + jnp.arange(kx_local, dtype=jnp.int32)).astype(
        jnp.float32
    )[:, None, None]
    modes_y = lax.axis_index("row") * ky_local + jnp.arange(ky_local, dtype=jnp.int32) - KC
    wave_y = jnp.broadcast_to(modes_y.astype(jnp.float32)[:, None], (ky_local, modes_z)).reshape(-1)
    z_values = (jnp.arange(modes_z, dtype=jnp.int32) - half_z).astype(jnp.float32) * (NX / total_z)
    wave_z = jnp.broadcast_to(z_values[None, :], (ky_local, modes_z)).reshape(-1)
    squared = wave_x * wave_x + wave_y * wave_y + wave_z * wave_z
    coeff_phase = spectra[:, 0]
    coeff_u = spectra[:, 1]
    coeff_v = spectra[:, 2]
    coeff_w = spectra[:, 3]
    gradients = [
        times_i(wave_x * coeff_phase),
        times_i(wave_y * coeff_phase),
        times_i(wave_z * coeff_phase),
    ]
    laplace = -squared * coeff_phase
    vortex_hat = [
        times_i(wave_y * coeff_w - wave_z * coeff_v),
        times_i(wave_z * coeff_u - wave_x * coeff_w),
        times_i(wave_x * coeff_v - wave_y * coeff_u),
    ]
    leading = inverse(jnp.stack(gradients + [laplace], axis=1))
    advect, bulk_term, potential = phase_terms(phase, velocity, leading[0:3], leading[3])
    phase_side = forward(jnp.stack([advect, bulk_term]))
    vortex = inverse(jnp.stack(vortex_hat, axis=1))
    flow_side = forward(momentum(velocity, vortex, leading[0:3], potential))
    nonlinear = jnp.concatenate([phase_side, flow_side], axis=1)
    mean_mode = (wave_x == 0) & (wave_y == 0) & (wave_z == 0)
    advect_hat = jnp.where(mean_mode, 0.0, nonlinear[:, 0])
    bulk_hat = nonlinear[:, 1]
    stable_part = 1.0 / time_step + mobility * stabilizer * squared
    new_phase = (stable_part * coeff_phase - advect_hat - mobility * squared * bulk_hat) / (
        stable_part + mobility * epsilon * epsilon * squared * squared
    )
    viscous = 1.0 / time_step + squared / reynolds
    unprojected = [
        (spectra[:, 1 + j] / time_step + nonlinear[:, 2 + j]) / viscous for j in range(3)
    ]
    normal_part = (
        wave_x * unprojected[0] + wave_y * unprojected[1] + wave_z * unprojected[2]
    ) / jnp.maximum(squared, 1.0)
    waves = [wave_x, wave_y, wave_z]
    new_flow = [unprojected[j] - waves[j] * normal_part for j in range(3)]
    result = inverse(jnp.stack([new_phase] + new_flow, axis=1))
    return (result[0], result[1:4])


def tables(cols, rows, rows_y, planes):
    total_z = planes * rows
    half_z = 3 * total_z // 8
    modes_z = 2 * half_z
    kx_row = KC // rows

    def pair(first, second, period):
        residue = first[:, None] * second[None, :] % period
        angles = residue.astype(np.float32) * np.float32(2.0 * math.pi / period)
        return [np.cos(angles).astype(ml_dtypes.bfloat16), np.sin(angles).astype(ml_dtypes.bfloat16)]

    cos_x, sin_x = pair(np.arange(KC), np.arange(NX), NX)
    cos_y, sin_y = pair(np.arange(NY), np.arange(KY) - KC, NY)
    cos_z, sin_z = pair(np.arange(total_z), np.arange(modes_z) - half_z, total_z)
    x_table = np.stack([cos_x, -sin_x]).reshape(2, rows, kx_row // 2, 2, NX)
    x_table = x_table.transpose(1, 0, 3, 2, 4).reshape(2 * KC, NX)
    y_forward = np.concatenate([cos_y, sin_y], axis=1)
    y_inverse = np.concatenate([cos_y.T, sin_y.T], axis=1)
    cz, sz = (t.reshape(rows, planes, modes_z) for t in (cos_z, sin_z))
    z_forward = np.stack([np.stack([cz, sz], 1), np.stack([-sz, cz], 1)])
    z_forward = z_forward.transpose(0, 4, 1, 2, 3).reshape(2 * modes_z, 2 * total_z)
    z_inverse = np.stack([np.stack([cz, -sz], 2), np.stack([sz, cz], 2)], 1)
    z_inverse = z_inverse.reshape(2 * total_z, 2 * modes_z)
    z_rotated = np.concatenate([z_inverse[:, modes_z:], -z_inverse[:, :modes_z]], axis=1)
    made = (x_table, y_forward, y_inverse, z_forward, z_inverse, z_rotated)
    return [jnp.asarray(t.astype(ml_dtypes.bfloat16)) for t in made]


def dot(first, second, dims=((1,), (0,))):
    return lax.dot_general(first, second, (dims, ((), ())), preferred_element_type=jnp.float32)


LANES = 128


def fast_device(sizes, phase, velocity):
    cols, rows, rows_y, planes = sizes
    total_z = planes * rows
    half_z = 3 * total_z // 8
    modes_z = 2 * half_z
    kx_row = KC // rows
    kx_own = kx_row // cols
    pairs = kx_row // 2
    points = rows_y * planes
    row_lanes = kx_row * rows_y
    col_lanes = kx_own * rows_y
    own = kx_own * modes_z
    scale_inv = 1.0 / (NX * NY * total_z)
    made_tables = tables(cols, rows, rows_y, planes)
    f32, bf16 = jnp.float32, jnp.bfloat16
    forward_count, derived_count, derived_lines, final_count = 9, 7, 6, 4
    row_count = forward_count + derived_count + final_count
    col_count = forward_count + derived_lines + final_count

    def exchange(axis, size, src, dst, send, recv):
        me = lax.axis_index(axis)

        def copy(f, d):
            peer = lax.rem(me + d, size)
            return pltpu.make_async_remote_copy(
                src_ref=src.at[f, peer],
                dst_ref=dst.at[f, me],
                send_sem=send.at[f, d - 1],
                recv_sem=recv.at[f, d - 1],
                device_id={axis: peer},
                device_id_type=pl.DeviceIdType.MESH,
            )

        def start(f):
            for d in range(1, size):
                copy(f, d).start()
            dst[f, me] = src[f, me]

        def arrived(f):
            for d in range(1, size):
                copy(f, d).wait_recv()

        def sent(f):
            for d in range(1, size):
                copy(f, d).wait_send()

        return start, arrived, sent

    def greet():
        barrier = pltpu.get_barrier_semaphore()
        for axis, size in (("col", cols), ("row", rows)):
            for d in range(1, size):
                peer = lax.rem(lax.axis_index(axis) + d, size)
                pl.semaphore_signal(
                    barrier, inc=1, device_id={axis: peer}, device_id_type=pl.DeviceIdType.MESH
                )
        pl.semaphore_wait(barrier, cols + rows - 2)

    def swap_halves(first, second):
        half = LANES // 2
        low = jnp.concatenate([first[:, :half], second[:, :half]], axis=1)
        high = jnp.concatenate([first[:, half:], second[:, half:]], axis=1)
        return low, high

    def body(*refs):
        phase_in, flow_in = refs[:2]
        table_in = refs[2:8]
        phase_out, flow_out = refs[8:10]
        (
            row_src, row_dst, col_src, col_dst, fields, lines, derived, coeff, ready,
            x_tab, yf_tab, yi_tab, zf_tab, zi_tab, zr_tab,
            row_send, row_recv, col_send, col_recv, load_sem, table_sem, store_sem,
        ) = refs[10:]
        table_refs = (x_tab, yf_tab, yi_tab, zf_tab, zi_tab, zr_tab)
        row_start, row_arrived, row_sent = exchange("row", rows, row_src, row_dst, row_send, row_recv)
        col_start, col_arrived, col_sent = exchange("col", cols, col_src, col_dst, col_send, col_recv)

        def load(j, z):
            source = phase_in.at[:, z, :] if j == 0 else flow_in.at[j - 1, :, z, :]
            target = fields.at[j, pl.ds(z * rows_y, rows_y), :]
            return pltpu.make_async_copy(source, target, load_sem.at[j, z])

        def store(j, z):
            target = phase_out.at[:, z, :] if j == 0 else flow_out.at[j - 1, :, z, :]
            source = derived.at[j, pl.ds(z * rows_y, rows_y), :]
            return pltpu.make_async_copy(source, target, store_sem.at[j, z])

        def table_copy(k):
            return pltpu.make_async_copy(table_in[k], table_refs[k], table_sem.at[k])

        first_kx = lax.axis_index("row") * kx_row
        own_kx = first_kx + lax.axis_index("col") * kx_own

        def x_forward(f):
            made = dot(x_tab[...], lines[f], ((1,), (1,)))
            for r in range(rows):
                parts = []
                for p in range(2):
                    base = (r * 2 + p) * kx_row
                    even = made[base : base + pairs]
                    odd = made[base + pairs : base + kx_row]
                    planes_made = []
                    for j in range(planes // 2):
                        at = slice(j * LANES, (j + 1) * LANES)
                        planes_made.extend(swap_halves(even[:, at], odd[:, at]))
                    parts.append(jnp.swapaxes(jnp.stack(planes_made), 0, 1))
                both = jnp.concatenate(parts, axis=1).astype(bf16)
                for k in range(pairs):
                    row_src[f, r, :, k * LANES : (k + 1) * LANES] = both[k]
            row_start(f)

        def x_inverse(h):
            row_arrived(h)
            made = []
            for r in range(rows):
                whole_lines = row_dst[h, r].astype(f32)
                tiles = jnp.stack([whole_lines[:, k * LANES : (k + 1) * LANES] for k in range(pairs)])
                for p in range(2):
                    by_plane = jnp.swapaxes(tiles[:, p * planes : (p + 1) * planes], 0, 1)
                    even, odd = [], []
                    for j in range(planes // 2):
                        low, high = swap_halves(by_plane[2 * j], by_plane[2 * j + 1])
                        even.append(low)
                        odd.append(high)
                    made.append(jnp.concatenate(even, axis=1))
                    made.append(jnp.concatenate(odd, axis=1))
            gathered = jnp.concatenate(made, axis=0).astype(bf16)
            return dot(gathered, x_tab[...], ((0,), (0,)))

        def z_forward(f):
            row_arrived(f)
            stacked = row_dst[f].reshape(2 * total_z, row_lanes)
            made = dot(zf_tab[...], stacked).astype(bf16)
            for c in range(cols):
                col_src[f, c] = made[:, c * col_lanes : (c + 1) * col_lanes]
            col_start(f)

        def joined(g):
            return jnp.concatenate([col_dst[g, c] for c in range(cols)], axis=1)

        def row_emit(h, made):
            made = made.astype(bf16)
            for r in range(rows):
                row_src[h, r] = made[r * 2 * planes : (r + 1) * 2 * planes]
            row_start(h)

        def z_inverse(g, h):
            col_arrived(g)
            row_emit(h, dot(zi_tab[...], joined(g)))

        def y_forward(f):
            col_arrived(f)
            lhs = jnp.concatenate(
                [
                    jnp.concatenate(
                        [col_dst[f, c, :, a * rows_y : (a + 1) * rows_y] for c in range(cols)], axis=1
                    )
                    for a in range(kx_own)
                ],
                axis=0,
            )
            made = dot(lhs, yf_tab[...]).reshape(kx_own, 2 * modes_z, 2 * KY)
            first, second = made[:, :modes_z], made[:, modes_z:]
            real = first[:, :, :KY] + second[:, :, KY:]
            imag = second[:, :, :KY] - first[:, :, KY:]
            coeff[f, 0] = real.reshape(own, KY) * scale_inv
            coeff[f, 1] = imag.reshape(own, KY) * scale_inv

        def y_inverse(e):
            made = dot(ready[e], yi_tab[...])
            first, second = made[:own], made[own:]
            real = (first[:, :NY] - second[:, NY:]).reshape(kx_own, modes_z, NY)
            imag = (first[:, NY:] + second[:, :NY]).reshape(kx_own, modes_z, NY)
            both = jnp.concatenate([real, imag], axis=1).astype(bf16)
            g = e + forward_count
            for c in range(cols):
                col_src[g, c] = jnp.concatenate(
                    [both[a, :, c * rows_y : (c + 1) * rows_y] for a in range(kx_own)], axis=1
                )
            col_start(g)

        block = 2 * modes_z

        def spectral(work):
            def step(i, carry):
                base = pl.multiple_of(i * block, block)
                at = pl.ds(base, block)
                row = lax.broadcasted_iota(jnp.int32, (block, KY), 0)
                upper = row >= modes_z
                kx = own_kx + 2 * i + jnp.where(upper, 1, 0)
                kz = jnp.where(upper, row - modes_z, row) - half_z
                ky = lax.broadcasted_iota(jnp.int32, (block, KY), 1) - KC
                weight = jnp.where(kx == 0, 1.0, 2.0)
                mean_mode = (kx == 0) & (ky == 0) & (kz == 0)
                wx, wy = kx.astype(f32), ky.astype(f32)
                wz = kz.astype(f32) * (NX / total_z)
                k2 = wx * wx + wy * wy + wz * wz

                def get(f):
                    return coeff[f, 0, at, :], coeff[f, 1, at, :]

                def put(e, real, imag):
                    ready[e, at, :] = (real * weight).astype(bf16)
                    ready[e, pl.ds(pl.multiple_of(own + base, block), block), :] = (
                        imag * weight
                    ).astype(bf16)

                work(get, put, wx, wy, wz, k2, mean_mode)
                return carry

            lax.fori_loop(0, own // block, step, 0)

        def derive_phase(get, put, wx, wy, wz, k2, mean_mode):
            real, imag = get(0)
            put(0, real, imag)
            put(1, -(wy * imag), wy * real)
            put(2, -k2 * real, -k2 * imag)

        def derive_vortex(get, put, wx, wy, wz, k2, mean_mode):
            w = [wx, wy, wz]
            got = [get(1 + j) for j in range(3)]
            for e, j in ((3, 2), (4, 1), (5, 0)):
                p, q = (j + 1) % 3, (j + 2) % 3
                real = -(w[p] * got[q][1] - w[q] * got[p][1])
                put(e, real, w[p] * got[q][0] - w[q] * got[p][0])

        def solve_phase(get, put, wx, wy, wz, k2, mean_mode):
            old, bulk_hat, advect_hat = get(0), get(4), get(5)
            stable = 1.0 / time_step + mobility * stabilizer * k2
            below = stable + mobility * epsilon * epsilon * k2 * k2
            made = []
            for p in range(2):
                kept = jnp.where(mean_mode, 0.0, advect_hat[p])
                made.append((stable * old[p] - kept - mobility * k2 * bulk_hat[p]) / below)
            put(6, made[0], made[1])

        def solve_flow(get, put, wx, wy, wz, k2, mean_mode):
            viscous = 1.0 / time_step + k2 / reynolds
            largest = jnp.maximum(k2, 1.0)
            w = [wx, wy, wz]
            old = [get(1 + j) for j in range(3)]
            added = [get(6 + j) for j in range(3)]
            made = [[], [], []]
            for p in range(2):
                free = [(old[j][p] / time_step + added[j][p]) / viscous for j in range(3)]
                normal = (wx * free[0] + wy * free[1] + wz * free[2]) / largest
                for j in range(3):
                    made[j].append(free[j] - w[j] * normal)
            for j in range(3):
                put(7 + j, made[j][0], made[j][1])

        cut = 32

        def pointwise(work):
            def step(i, carry):
                work(pl.ds(pl.multiple_of(i * cut, cut), cut))
                return carry

            lax.fori_loop(0, points // cut, step, 0)

        def loop(begin, end, work):
            def step(i, carry):
                work(i)
                return carry

            lax.fori_loop(begin, end, step, 0)

        for z in range(planes):
            load(0, z).start()
        table_copy(0).start()
        for k in (3, 1, 2, 4, 5):
            table_copy(k).start()
        for j in range(1, 4):
            for z in range(planes):
                load(j, z).start()
        greet()

        def bring(f):
            def cast(at):
                lines[f, at, :] = fields[f, at, :].astype(bf16)

            pointwise(cast)
            x_forward(f)

        table_copy(0).wait()
        for j in range(4):
            for z in range(planes):
                load(j, z).wait()
        for k in range(1, 6):
            table_copy(k).wait()
        loop(0, 4, bring)

        def make_bulk(at):
            c = fields[0, at, :]
            lines[4, at, :] = (c * c * c - c).astype(bf16)

        pointwise(make_bulk)
        x_forward(4)
        loop(0, 4, z_forward)
        y_forward(0)
        spectral(derive_phase)
        loop(0, 3, y_inverse)
        loop(1, 4, y_forward)
        spectral(derive_vortex)
        loop(3, 6, y_inverse)
        z_forward(4)

        g0 = forward_count
        h0 = forward_count

        def phase_planes():
            col_arrived(g0)
            data = joined(g0)
            lane_kx = lax.broadcasted_iota(jnp.int32, (1, row_lanes), 1) // rows_y + first_kx
            row_emit(h0, dot(zr_tab[...], data) * lane_kx.astype(f32))
            row = lax.broadcasted_iota(jnp.int32, (2 * modes_z, 1), 0)
            kz = jnp.where(row >= modes_z, row - modes_z, row) - half_z
            scaled = (data.astype(f32) * (kz.astype(f32) * (NX / total_z))).astype(bf16)
            row_emit(h0 + 1, dot(zr_tab[...], scaled))

        def to_field(i):
            derived[i] = x_inverse(h0 + i)

        def make_advect(at):
            lines[5, at, :] = (
                fields[1, at, :] * derived[0, at, :]
                + fields[2, at, :] * derived[2, at, :]
                + fields[3, at, :] * derived[1, at, :]
            ).astype(bf16)

        gradient_at = (0, 2, 1)
        vortex_at = (6, 5, 4)

        def make_forcing(which):
            def work(at):
                c = fields[0, at, :]
                potential = c * c * c - c - epsilon * epsilon * derived[3, at, :]
                for j in which:
                    p, q = (j + 1) % 3, (j + 2) % 3
                    lines[6 + j, at, :] = (
                        fields[1 + p, at, :] * derived[vortex_at[q], at, :]
                        - fields[1 + q, at, :] * derived[vortex_at[p], at, :]
                        + potential * derived[gradient_at[j], at, :]
                    ).astype(bf16)

            return work

        phase_planes()
        z_inverse(g0 + 1, h0 + 2)
        loop(0, 2, to_field)
        z_inverse(g0 + 2, h0 + 3)
        to_field(2)
        pointwise(make_advect)
        x_forward(5)
        to_field(3)
        z_inverse(g0 + 3, h0 + 4)
        z_forward(5)
        to_field(4)
        z_inverse(g0 + 4, h0 + 5)
        to_field(5)
        pointwise(make_forcing((0,)))
        x_forward(6)
        z_inverse(g0 + 5, h0 + 6)
        z_forward(6)
        to_field(6)
        pointwise(make_forcing((1, 2)))
        loop(7, 9, x_forward)
        loop(4, 6, y_forward)
        spectral(solve_phase)
        y_inverse(6)
        loop(7, 9, z_forward)
        loop(6, 9, y_forward)
        spectral(solve_flow)
        loop(7, 10, y_inverse)

        g1 = forward_count + derived_lines
        h1 = forward_count + derived_count
        z_inverse(g1, h1)

        def finish(j):
            derived[j] = x_inverse(h1 + j)

        for j in range(final_count):
            if j + 1 < final_count:
                z_inverse(g1 + j + 1, h1 + j + 1)
            finish(j)
            for z in range(planes):
                store(j, z).start()
        loop(0, row_count, row_sent)
        loop(0, col_count, col_sent)
        for j in range(final_count):
            for z in range(planes):
                store(j, z).wait()

    sems = pltpu.SemaphoreType.DMA
    row_shape = (row_count, rows, 2 * planes, row_lanes)
    col_shape = (col_count, cols, 2 * modes_z, col_lanes)
    scratch = [
        pltpu.VMEM(row_shape, bf16),
        pltpu.VMEM(row_shape, bf16),
        pltpu.VMEM(col_shape, bf16),
        pltpu.VMEM(col_shape, bf16),
        pltpu.VMEM((4, points, NX), f32),
        pltpu.VMEM((forward_count, points, NX), bf16),
        pltpu.VMEM((derived_count, points, NX), f32),
        pltpu.VMEM((forward_count, 2, own, KY), f32),
        pltpu.VMEM((derived_lines + final_count, 2 * own, KY), bf16),
    ]
    scratch += [pltpu.VMEM(t.shape, bf16) for t in made_tables]
    scratch += [
        sems((row_count, rows - 1)),
        sems((row_count, rows - 1)),
        sems((col_count, cols - 1)),
        sems((col_count, cols - 1)),
        sems((4, planes)),
        sems((len(made_tables),)),
        sems((4, planes)),
    ]
    hbm = pl.BlockSpec(memory_space=pltpu.HBM)
    return tuple(
        pl.pallas_call(
            body,
            in_specs=[hbm] * (2 + len(made_tables)),
            out_specs=[hbm, hbm],
            out_shape=[
                jax.ShapeDtypeStruct(phase.shape, f32),
                jax.ShapeDtypeStruct(velocity.shape, f32),
            ],
            scratch_shapes=scratch,
            compiler_params=pltpu.CompilerParams(
                collective_id=0, has_side_effects=True, vmem_limit_bytes=67_043_328
            ),
            cost_estimate=pl.CostEstimate(
                flops=8_000_000_000, bytes_accessed=1 << 23, transcendentals=0
            ),
        )(phase, velocity, *made_tables)
    )


def solution(mesh):
    cols, rows = mesh.shape["col"], mesh.shape["row"]

    def on_device(phase, velocity):
        rows_y, planes = phase.shape[0], phase.shape[1]
        kx_own = KC // (rows * cols)
        modes_z = 2 * (3 * planes * rows // 8)
        aligned = planes == 8 and 2 * rows_y == LANES and cols % 2 == 0
        exact = KC == kx_own * rows * cols and kx_own % 2 == 0 and modes_z % 8 == 0
        if aligned and exact:
            return fast_device((cols, rows, rows_y, planes), phase, velocity)
        return plain_device(phase, velocity)

    return jax.shard_map(
        on_device,
        mesh=mesh,
        in_specs=(P("col", "row", None), P(None, "col", "row", None)),
        out_specs=(P("col", "row", None), P(None, "col", "row", None)),
        check_vma=False,
    )
```

time: 232 us -> 167 us (0.72)
  Pallas kernels: 221 us -> 159 us
  other arithmetic: 2.8 us -> 0 us
    pallas_call x8 -> x1, Pallas kernels: 221 us -> 159 us  [fast_device(): pl.pallas_call(body, in_specs=[hbm] * (2 + len(made_tables)), out_specs=[...]
    unnamed x25 -> x2, local copies, waits for them, and re-layouts: 5.96 us -> 6.12 us
where the time goes in v1:
time: 167 us; the launch traced here: 166 us
  Pallas kernels  159 us (95%)
  local copies, waits for them, and re-layouts  6.12 us (4%)
    pallas_call x1, Pallas kernels, fast_device(): pl.pallas_call(body, in_specs=[hbm] * (2 + len(made_tables)), out_specs=[...  159 us
    unnamed x2, local copies, waits for them, and re-layouts  6.12 us

profile of v1, /device:TPU:0, one launch (start us, length us, event | category | flops | bytes accessed | tf_op | source)
XLA Modules:
  0.0 165.8 jit_solution(17000754551969949053)
XLA Ops:
  0.6 159.1 %shard_map.95 = (f32[64,8,512]{2,1,0:T(8,128)}, f32[3,64,8,512]{3,2,1,0:T(8,128)}) custom-call(f32[64,8,512]{2,1,0:T(8,128)} %refs_0_.1, f32[3,64,8,512]{3,2,1,0:T(8,128)} %refs_1_.1, bf16[384,512]{1,0:T(8,128)(2,1)} %constant.12.clone.refs_2_, bf16[512,768]{1,0:T(8,128)(2,1)} %constant.13.clone.refs_3_, bf16[384,1024]{1,0:T(8,128)(2,1)} %constant.14.clone.refs_4_, ...), custom_call_target="tpu_custom_call" | custom-call | flops 8000000000 | bytes 8388608 | tf_op jit(solution)/shard_map/pallas_call | solution.py:648
  159.7 2.3 %copy.12 = f32[64,8,512]{2,1,0:T(8,128)} copy(f32[64,8,512]{2,1,0:T(8,128)} %get-tuple-element.4) | data formatting | bytes 2097152
  162.0 3.9 %copy.13 = f32[3,64,8,512]{3,2,1,0:T(8,128)} copy(f32[3,64,8,512]{3,2,1,0:T(8,128)} %get-tuple-element.5) | data formatting | bytes 6291456

commit v2 on v1

--- a/solution.py
+++ b/solution.py
@@ -204,17 +204,17 @@
     cos_x, sin_x = pair(np.arange(KC), np.arange(NX), NX)
     cos_y, sin_y = pair(np.arange(NY), np.arange(KY) - KC, NY)
     cos_z, sin_z = pair(np.arange(total_z), np.arange(modes_z) - half_z, total_z)
-    x_table = np.stack([cos_x, -sin_x]).reshape(2, rows, kx_row // 2, 2, NX)
+    order = np.arange(KC).reshape(cols, rows, kx_row // cols).transpose(1, 0, 2).reshape(KC)
+    x_table = np.stack([cos_x[order], -sin_x[order]]).reshape(2, rows, kx_row // 2, 2, NX)
     x_table = x_table.transpose(1, 0, 3, 2, 4).reshape(2 * KC, NX)
     y_forward = np.concatenate([cos_y, sin_y], axis=1)
-    y_inverse = np.concatenate([cos_y.T, sin_y.T], axis=1)
     cz, sz = (t.reshape(rows, planes, modes_z) for t in (cos_z, sin_z))
     z_forward = np.stack([np.stack([cz, sz], 1), np.stack([-sz, cz], 1)])
     z_forward = z_forward.transpose(0, 4, 1, 2, 3).reshape(2 * modes_z, 2 * total_z)
     z_inverse = np.stack([np.stack([cz, -sz], 2), np.stack([sz, cz], 2)], 1)
     z_inverse = z_inverse.reshape(2 * total_z, 2 * modes_z)
     z_rotated = np.concatenate([z_inverse[:, modes_z:], -z_inverse[:, :modes_z]], axis=1)
-    made = (x_table, y_forward, y_inverse, z_forward, z_inverse, z_rotated)
+    made = (x_table, y_forward, z_forward, z_inverse, z_rotated)
     return [jnp.asarray(t.astype(ml_dtypes.bfloat16)) for t in made]
 
 
@@ -240,9 +240,11 @@
     scale_inv = 1.0 / (NX * NY * total_z)
     made_tables = tables(cols, rows, rows_y, planes)
     f32, bf16 = jnp.float32, jnp.bfloat16
-    forward_count, derived_count, derived_lines, final_count = 9, 7, 6, 4
-    row_count = forward_count + derived_count + final_count
-    col_count = forward_count + derived_lines + final_count
+    forward_count, derived_count, derived_lines, final_count = 8, 7, 6, 3
+    row_count = forward_count + derived_count
+    col_count = forward_count + derived_lines
+    kx_col = kx_own * rows
+    wide_lanes = kx_own * KY
 
     def exchange(axis, size, src, dst, send, recv):
         me = lax.axis_index(axis)
@@ -281,7 +283,9 @@
                 pl.semaphore_signal(
                     barrier, inc=1, device_id={axis: peer}, device_id_type=pl.DeviceIdType.MESH
                 )
-        pl.semaphore_wait(barrier, cols + rows - 2)
+
+    def greeted():
+        pl.semaphore_wait(pltpu.get_barrier_semaphore(), cols + rows - 2)
 
     def swap_halves(first, second):
         half = LANES // 2
@@ -291,16 +295,24 @@
 
     def body(*refs):
         phase_in, flow_in = refs[:2]
-        table_in = refs[2:8]
-        phase_out, flow_out = refs[8:10]
+        table_in = refs[2:7]
+        phase_out, flow_out = refs[7:9]
         (
-            row_src, row_dst, col_src, col_dst, fields, lines, derived, coeff, ready,
-            x_tab, yf_tab, yi_tab, zf_tab, zi_tab, zr_tab,
-            row_send, row_recv, col_send, col_recv, load_sem, table_sem, store_sem,
-        ) = refs[10:]
-        table_refs = (x_tab, yf_tab, yi_tab, zf_tab, zi_tab, zr_tab)
+            row_src, row_dst, col_src, col_dst, thin_src, thin_dst, wide_src, wide_dst,
+            fields, lines, derived, coeff, ready,
+            x_tab, yf_tab, zf_tab, zi_tab, zr_tab, xw_tab, yi_tab,
+            row_send, row_recv, col_send, col_recv, thin_send, thin_recv, wide_send, wide_recv,
+            load_sem, table_sem, store_sem,
+        ) = refs[9:]
+        table_refs = (x_tab, yf_tab, zf_tab, zi_tab, zr_tab)
         row_start, row_arrived, row_sent = exchange("row", rows, row_src, row_dst, row_send, row_recv)
         col_start, col_arrived, col_sent = exchange("col", cols, col_src, col_dst, col_send, col_recv)
+        thin_start, thin_arrived, thin_sent = exchange(
+            "row", rows, thin_src, thin_dst, thin_send, thin_recv
+        )
+        wide_start, wide_arrived, wide_sent = exchange(
+            "col", cols, wide_src, wide_dst, wide_send, wide_recv
+        )
 
         def load(j, z):
             source = phase_in.at[:, z, :] if j == 0 else flow_in.at[j - 1, :, z, :]
@@ -315,11 +327,11 @@
         def table_copy(k):
             return pltpu.make_async_copy(table_in[k], table_refs[k], table_sem.at[k])
 
-        first_kx = lax.axis_index("row") * kx_row
-        own_kx = first_kx + lax.axis_index("col") * kx_own
+        row_kx = lax.axis_index("row") * kx_own
+        own_kx = lax.axis_index("col") * kx_col + row_kx
 
         def x_forward(f):
-            made = dot(x_tab[...], lines[f], ((1,), (1,)))
+            made = dot(x_tab[...], lines[lax.rem(f, 5)], ((1,), (1,)))
             for r in range(rows):
                 parts = []
                 for p in range(2):
@@ -333,8 +345,8 @@
                     parts.append(jnp.swapaxes(jnp.stack(planes_made), 0, 1))
                 both = jnp.concatenate(parts, axis=1).astype(bf16)
                 for k in range(pairs):
-                    row_src[f, r, :, k * LANES : (k + 1) * LANES] = both[k]
-            row_start(f)
+                    row_src[f - 1, r, :, k * LANES : (k + 1) * LANES] = both[k]
+            row_start(f - 1)
 
         def x_inverse(h):
             row_arrived(h)
@@ -355,12 +367,12 @@
             return dot(gathered, x_tab[...], ((0,), (0,)))
 
         def z_forward(f):
-            row_arrived(f)
-            stacked = row_dst[f].reshape(2 * total_z, row_lanes)
+            row_arrived(f - 1)
+            stacked = row_dst[f - 1].reshape(2 * total_z, row_lanes)
             made = dot(zf_tab[...], stacked).astype(bf16)
             for c in range(cols):
-                col_src[f, c] = made[:, c * col_lanes : (c + 1) * col_lanes]
-            col_start(f)
+                col_src[f - 1, c] = made[:, c * col_lanes : (c + 1) * col_lanes]
+            col_start(f - 1)
 
         def joined(g):
             return jnp.concatenate([col_dst[g, c] for c in range(cols)], axis=1)
@@ -371,16 +383,108 @@
                 row_src[h, r] = made[r * 2 * planes : (r + 1) * 2 * planes]
             row_start(h)
 
+        def wide_tables():
+            out_row = lax.broadcasted_iota(jnp.int32, (2 * KC, 2 * KC), 0)
+            in_row = lax.broadcasted_iota(jnp.int32, (2 * KC, 2 * KC), 1)
+            c = out_row // (2 * kx_col)
+            inside = out_row - c * 2 * kx_col
+            part = jnp.where(inside >= kx_col, 1, 0)
+            kx = inside - part * kx_col
+            r = kx // kx_own
+            a = c * kx_own + kx - r * kx_own
+            wanted = (2 * r + part) * kx_row + (a % 2) * pairs + a // 2
+            chosen = jnp.where(in_row == wanted, 1.0, 0.0).astype(bf16)
+            xw_tab[...] = dot(chosen, x_tab[...]).astype(bf16)
+
+        def inverse_table():
+            for t in range(2):
+                part = yf_tab[:, t * KY : (t + 1) * KY].astype(f32)
+                yi_tab[:, t * NY : (t + 1) * NY] = part.T.astype(bf16)
+
+        def first_x():
+            made = dot(xw_tab[...], lines[0], ((1,), (1,))).astype(bf16)
+            wide_src[0] = made.reshape(cols, 2 * kx_col, points)
+
+        def first_y():
+            wide_arrived(0)
+            lhs = jnp.concatenate(
+                [
+                    jnp.concatenate(
+                        [wide_dst[0, c, :, z * rows_y : (z + 1) * rows_y] for c in range(cols)], axis=1
+                    )
+                    for z in range(planes)
+                ],
+                axis=0,
+            )
+            made = dot(lhs, yf_tab[...]).reshape(planes, 2 * kx_col, 2 * KY)
+            first, second = made[:, :kx_col], made[:, kx_col:]
+            real = jnp.swapaxes(first[:, :, :KY] + second[:, :, KY:], 0, 1)
+            imag = jnp.swapaxes(second[:, :, :KY] - first[:, :, KY:], 0, 1)
+            both = jnp.concatenate([real, imag], axis=1).astype(bf16)
+            for k in range(kx_col):
+                r, a = k // kx_own, k % kx_own
+                thin_src[0, r, :, a * KY : (a + 1) * KY] = both[k]
+            thin_start(0)
+
+        def first_z():
+            thin_arrived(0)
+            stacked = thin_dst[0].reshape(2 * total_z, wide_lanes)
+            made = dot(zf_tab[...], stacked) * scale_inv
+            for p in range(2):
+                for a in range(kx_own):
+                    coeff[0, p, a * modes_z : (a + 1) * modes_z, :] = made[
+                        p * modes_z : (p + 1) * modes_z, a * KY : (a + 1) * KY
+                    ]
+
+        def last_z():
+            parts = []
+            for p in range(2):
+                parts.append(
+                    jnp.concatenate(
+                        [coeff[0, p, a * modes_z : (a + 1) * modes_z, :] for a in range(kx_own)], axis=1
+                    )
+                )
+            made = dot(zi_tab[...], jnp.concatenate(parts, axis=0).astype(bf16)).astype(bf16)
+            for r in range(rows):
+                thin_src[0, r] = made[r * 2 * planes : (r + 1) * 2 * planes]
+            thin_start(0)
+
+        def last_y():
+            thin_arrived(0)
+            lhs = jnp.concatenate(
+                [
+                    thin_dst[0, r, :, a * KY : (a + 1) * KY]
+                    for r in range(rows)
+                    for a in range(kx_own)
+                ],
+                axis=0,
+            )
+            made = dot(lhs, yi_tab[...]).reshape(kx_col, 2 * planes, 2 * NY)
+            first, second = made[:, :planes], made[:, planes:]
+            real = jnp.swapaxes(first[:, :, :NY] - second[:, :, NY:], 0, 1)
+            imag = jnp.swapaxes(first[:, :, NY:] + second[:, :, :NY], 0, 1)
+            both = jnp.concatenate([real, imag], axis=1).astype(bf16)
+            for c in range(cols):
+                wide_src[0, c] = jnp.concatenate(
+                    [both[z, :, c * rows_y : (c + 1) * rows_y] for z in range(planes)], axis=1
+                )
+            wide_start(0)
+
+        def last_x():
+            wide_arrived(0)
+            gathered = wide_dst[0].reshape(2 * KC, points)
+            return dot(gathered, xw_tab[...], ((0,), (0,)))
+
         def z_inverse(g, h):
             col_arrived(g)
             row_emit(h, dot(zi_tab[...], joined(g)))
 
         def y_forward(f):
-            col_arrived(f)
+            col_arrived(f - 1)
             lhs = jnp.concatenate(
                 [
                     jnp.concatenate(
-                        [col_dst[f, c, :, a * rows_y : (a + 1) * rows_y] for c in range(cols)], axis=1
+                        [col_dst[f - 1, c, :, a * rows_y : (a + 1) * rows_y] for c in range(cols)], axis=1
                     )
                     for a in range(kx_own)
                 ],
@@ -393,13 +497,12 @@
             coeff[f, 0] = real.reshape(own, KY) * scale_inv
             coeff[f, 1] = imag.reshape(own, KY) * scale_inv
 
-        def y_inverse(e):
+        def y_inverse(e, g):
             made = dot(ready[e], yi_tab[...])
             first, second = made[:own], made[own:]
             real = (first[:, :NY] - second[:, NY:]).reshape(kx_own, modes_z, NY)
             imag = (first[:, NY:] + second[:, :NY]).reshape(kx_own, modes_z, NY)
             both = jnp.concatenate([real, imag], axis=1).astype(bf16)
-            g = e + forward_count
             for c in range(cols):
                 col_src[g, c] = jnp.concatenate(
                     [both[a, :, c * rows_y : (c + 1) * rows_y] for a in range(kx_own)], axis=1
@@ -427,6 +530,10 @@
                     return coeff[f, 0, at, :], coeff[f, 1, at, :]
 
                 def put(e, real, imag):
+                    if e is None:
+                        coeff[0, 0, at, :] = real * weight
+                        coeff[0, 1, at, :] = imag * weight
+                        return
                     ready[e, at, :] = (real * weight).astype(bf16)
                     ready[e, pl.ds(pl.multiple_of(own + base, block), block), :] = (
                         imag * weight
@@ -459,7 +566,7 @@
             for p in range(2):
                 kept = jnp.where(mean_mode, 0.0, advect_hat[p])
                 made.append((stable * old[p] - kept - mobility * k2 * bulk_hat[p]) / below)
-            put(6, made[0], made[1])
+            put(0, made[0], made[1])
 
         def solve_flow(get, put, wx, wy, wz, k2, mean_mode):
             viscous = 1.0 / time_step + k2 / reynolds
@@ -474,7 +581,7 @@
                 for j in range(3):
                     made[j].append(free[j] - w[j] * normal)
             for j in range(3):
-                put(7 + j, made[j][0], made[j][1])
+                put(1 + j if j < 2 else None, made[j][0], made[j][1])
 
         cut = 32
 
@@ -494,42 +601,54 @@
 
         for z in range(planes):
             load(0, z).start()
-        table_copy(0).start()
-        for k in (3, 1, 2, 4, 5):
+        for k in range(len(table_refs)):
             table_copy(k).start()
         for j in range(1, 4):
             for z in range(planes):
                 load(j, z).start()
         greet()
 
+        def cast(f):
+            def work(at):
+                lines[f, at, :] = fields[f, at, :].astype(bf16)
+
+            pointwise(work)
+
         def bring(f):
-            def cast(at):
-                lines[f, at, :] = fields[f, at, :].astype(bf16)
-
-            pointwise(cast)
-            x_forward(f)
-
-        table_copy(0).wait()
-        for j in range(4):
             for z in range(planes):
-                load(j, z).wait()
-        for k in range(1, 6):
-            table_copy(k).wait()
-        loop(0, 4, bring)
+                load(f, z).wait()
+            cast(f)
 
         def make_bulk(at):
             c = fields[0, at, :]
             lines[4, at, :] = (c * c * c - c).astype(bf16)
 
+        def send_derived(e):
+            y_inverse(e, forward_count + e)
+
+        table_copy(0).wait()
+        wide_tables()
+        bring(0)
+        first_x()
+        greeted()
+        wide_start(0)
+        for j in range(1, 4):
+            bring(j)
+        loop(1, 4, x_forward)
+        for k in range(1, len(table_refs)):
+            table_copy(k).wait()
+        inverse_table()
         pointwise(make_bulk)
+        loop(1, 3, z_forward)
+        first_y()
         x_forward(4)
-        loop(0, 4, z_forward)
-        y_forward(0)
+        z_forward(3)
+        first_z()
         spectral(derive_phase)
-        loop(0, 3, y_inverse)
+        loop(0, 3, send_derived)
         loop(1, 4, y_forward)
         spectral(derive_vortex)
-        loop(3, 6, y_inverse)
+        loop(3, 6, send_derived)
         z_forward(4)
 
         g0 = forward_count
@@ -538,7 +657,9 @@
         def phase_planes():
             col_arrived(g0)
             data = joined(g0)
-            lane_kx = lax.broadcasted_iota(jnp.int32, (1, row_lanes), 1) // rows_y + first_kx
+            at_lane = lax.broadcasted_iota(jnp.int32, (1, row_lanes), 1)
+            owner = at_lane // col_lanes
+            lane_kx = owner * (kx_col - kx_own) + at_lane // rows_y + row_kx
             row_emit(h0, dot(zr_tab[...], data) * lane_kx.astype(f32))
             row = lax.broadcasted_iota(jnp.int32, (2 * modes_z, 1), 0)
             kz = jnp.where(row >= modes_z, row - modes_z, row) - half_z
@@ -549,7 +670,7 @@
             derived[i] = x_inverse(h0 + i)
 
         def make_advect(at):
-            lines[5, at, :] = (
+            lines[0, at, :] = (
                 fields[1, at, :] * derived[0, at, :]
                 + fields[2, at, :] * derived[2, at, :]
                 + fields[3, at, :] * derived[1, at, :]
@@ -564,7 +685,7 @@
                 potential = c * c * c - c - epsilon * epsilon * derived[3, at, :]
                 for j in which:
                     p, q = (j + 1) % 3, (j + 2) % 3
-                    lines[6 + j, at, :] = (
+                    lines[1 + j, at, :] = (
                         fields[1 + p, at, :] * derived[vortex_at[q], at, :]
                         - fields[1 + q, at, :] * derived[vortex_at[p], at, :]
                         + potential * derived[gradient_at[j], at, :]
@@ -579,88 +700,136 @@
         to_field(2)
         pointwise(make_advect)
         x_forward(5)
+        z_inverse(g0 + 3, h0 + 4)
         to_field(3)
-        z_inverse(g0 + 3, h0 + 4)
         z_forward(5)
+        z_inverse(g0 + 4, h0 + 5)
         to_field(4)
-        z_inverse(g0 + 4, h0 + 5)
+        z_inverse(g0 + 5, h0 + 6)
         to_field(5)
         pointwise(make_forcing((0,)))
         x_forward(6)
-        z_inverse(g0 + 5, h0 + 6)
-        z_forward(6)
         to_field(6)
         pointwise(make_forcing((1, 2)))
         loop(7, 9, x_forward)
+        z_forward(6)
         loop(4, 6, y_forward)
         spectral(solve_phase)
-        y_inverse(6)
         loop(7, 9, z_forward)
+        loop(0, final_count, row_sent)
+        loop(0, final_count, col_sent)
+        thin_sent(0)
+        wide_sent(0)
+        y_inverse(0, 0)
         loop(6, 9, y_forward)
         spectral(solve_flow)
-        loop(7, 10, y_inverse)
-
-        g1 = forward_count + derived_lines
-        h1 = forward_count + derived_count
-        z_inverse(g1, h1)
+        last_z()
+        def send_flow(e):
+            y_inverse(e, e)
+
+        loop(1, final_count, send_flow)
+        last_y()
+
+        z_inverse(0, 0)
 
         def finish(j):
-            derived[j] = x_inverse(h1 + j)
-
-        for j in range(final_count):
-            if j + 1 < final_count:
-                z_inverse(g1 + j + 1, h1 + j + 1)
-            finish(j)
+            z_inverse(j + 1, j + 1)
+            derived[j] = x_inverse(j)
+
+        def emit(j):
             for z in range(planes):
                 store(j, z).start()
+
+        loop(0, 2, finish)
+        emit(0)
+        emit(1)
+        derived[2] = x_inverse(2)
+        emit(2)
+        derived[3] = last_x()
+        emit(3)
         loop(0, row_count, row_sent)
         loop(0, col_count, col_sent)
-        for j in range(final_count):
+        thin_sent(0)
+        wide_sent(0)
+        for j in range(4):
             for z in range(planes):
                 store(j, z).wait()
 
     sems = pltpu.SemaphoreType.DMA
     row_shape = (row_count, rows, 2 * planes, row_lanes)
     col_shape = (col_count, cols, 2 * modes_z, col_lanes)
-    scratch = [
-        pltpu.VMEM(row_shape, bf16),
-        pltpu.VMEM(row_shape, bf16),
-        pltpu.VMEM(col_shape, bf16),
-        pltpu.VMEM(col_shape, bf16),
+    thin_shape = (1, rows, 2 * planes, wide_lanes)
+    wide_shape = (1, cols, 2 * kx_col, points)
+    scratch = []
+    for shape in (row_shape, col_shape, thin_shape, wide_shape):
+        scratch += [pltpu.VMEM(shape, bf16), pltpu.VMEM(shape, bf16)]
+    scratch += [
         pltpu.VMEM((4, points, NX), f32),
-        pltpu.VMEM((forward_count, points, NX), bf16),
+        pltpu.VMEM((5, points, NX), bf16),
         pltpu.VMEM((derived_count, points, NX), f32),
-        pltpu.VMEM((forward_count, 2, own, KY), f32),
-        pltpu.VMEM((derived_lines + final_count, 2 * own, KY), bf16),
+        pltpu.VMEM((9, 2, own, KY), f32),
+        pltpu.VMEM((derived_lines, 2 * own, KY), bf16),
     ]
     scratch += [pltpu.VMEM(t.shape, bf16) for t in made_tables]
-    scratch += [
-        sems((row_count, rows - 1)),
-        sems((row_count, rows - 1)),
-        sems((col_count, cols - 1)),
-        sems((col_count, cols - 1)),
-        sems((4, planes)),
-        sems((len(made_tables),)),
-        sems((4, planes)),
+    scratch += [pltpu.VMEM((2 * KC, NX), bf16), pltpu.VMEM((KY, 2 * NY), bf16)]
+    for shape, size in ((row_shape, rows), (col_shape, cols), (thin_shape, rows), (wide_shape, cols)):
+        scratch += [sems((shape[0], size - 1)), sems((shape[0], size - 1))]
+    scratch += [sems((4, planes)), sems((len(made_tables),)), sems((4, planes))]
+    hbm = pl.BlockSpec(memory_space=pltpu.HBM)
+    out_shape = [
+        jax.ShapeDtypeStruct(phase.shape, f32),
+        jax.ShapeDtypeStruct(velocity.shape, f32),
     ]
-    hbm = pl.BlockSpec(memory_space=pltpu.HBM)
+    result = pl.pallas_call(
+        body,
+        in_specs=[hbm] * (2 + len(made_tables)),
+        out_specs=[hbm, hbm],
+        out_shape=out_shape,
+        scratch_shapes=scratch,
+        compiler_params=pltpu.CompilerParams(
+            collective_id=0, has_side_effects=True, vmem_limit_bytes=67_043_328
+        ),
+        cost_estimate=pl.CostEstimate(
+            flops=8_000_000_000, bytes_accessed=1 << 23, transcendentals=0
+        ),
+    )(phase, velocity, *made_tables)
+
+    cuts = 4
+    part = rows_y // cuts
+
+    def deliver(phase_in, flow_in, phase_out, flow_out, held, load_sem, store_sem):
+        def copies(j, k):
+            at = pl.ds(k * part, part)
+            source = phase_in.at[at] if j == 0 else flow_in.at[j - 1, at]
+            target = phase_out.at[at] if j == 0 else flow_out.at[j - 1, at]
+            load = pltpu.make_async_copy(source, held.at[j, at], load_sem.at[j, k])
+            return load, pltpu.make_async_copy(held.at[j, at], target, store_sem.at[j, k])
+
+        for j in range(4):
+            for k in range(cuts):
+                copies(j, k)[0].start()
+        for j in range(4):
+            for k in range(cuts):
+                copies(j, k)[0].wait()
+                copies(j, k)[1].start()
+        for j in range(4):
+            for k in range(cuts):
+                copies(j, k)[1].wait()
+
     return tuple(
         pl.pallas_call(
-            body,
-            in_specs=[hbm] * (2 + len(made_tables)),
+            deliver,
+            in_specs=[hbm, hbm],
             out_specs=[hbm, hbm],
-            out_shape=[
-                jax.ShapeDtypeStruct(phase.shape, f32),
-                jax.ShapeDtypeStruct(velocity.shape, f32),
+            out_shape=out_shape,
+            scratch_shapes=[
+                pltpu.VMEM((4,) + phase.shape, f32), sems((4, cuts)), sems((4, cuts)),
             ],
-            scratch_shapes=scratch,
-            compiler_params=pltpu.CompilerParams(
-                collective_id=0, has_side_effects=True, vmem_limit_bytes=67_043_328
+            compiler_params=pltpu.CompilerParams(vmem_limit_bytes=67_043_328),
+            cost_estimate=pl.CostEstimate(
+                flops=1_000_000, bytes_accessed=1 << 23, transcendentals=0
             ),
-            cost_estimate=pl.CostEstimate(
-                flops=8_000_000_000, bytes_accessed=1 << 23, transcendentals=0
-            ),
-        )(phase, velocity, *made_tables)
+        )(*result)
     )
 
 

time: 167 us -> 152 us (0.910)
  the two profiles are of different devices: /device:TPU:0 before, /device:TPU:27 now
where the time goes in v2:
time: 152 us
  Pallas kernels  151 us (99%)
    pallas_call x1, Pallas kernels, fast_device(): pl.pallas_call(body, in_specs=[hbm] * (2 + len(made_tables)), out_specs=[...  147 us
    pallas_call x1, Pallas kernels, fast_device(): pl.pallas_call(deliver, in_specs=[hbm, hbm], out_specs=[hbm, hbm], out_sh...  3.85 us

profile of v2, /device:TPU:27, one launch (start us, length us, event | category | flops | bytes accessed | tf_op | source)
XLA Modules:
  0.0 151.9 jit_solution(6851100432072842230)
XLA Ops:
  0.6 147.3 %shard_map.86 = (f32[64,8,512]{2,1,0:T(8,128)}, f32[3,64,8,512]{3,2,1,0:T(8,128)}) custom-call(f32[64,8,512]{2,1,0:T(8,128)} %refs_0_.1, f32[3,64,8,512]{3,2,1,0:T(8,128)} %refs_1_.1, bf16[384,512]{1,0:T(8,128)(2,1)} %constant.10.clone.refs_2_, bf16[512,768]{1,0:T(8,128)(2,1)} %constant.11.clone.refs_3_, bf16[48,64]{1,0:T(8,128)(2,1)} %constant.12.clone.refs_4_, ...), custom_call_target="tpu_custom_call" | custom-call | flops 8000000000 | bytes 8388608 | tf_op jit(solution)/shard_map/pallas_call | solution.py:783
  147.9 3.9 %shard_map.87 = (f32[64,8,512]{2,1,0:T(8,128)}, f32[3,64,8,512]{3,2,1,0:T(8,128)}) custom-call(f32[64,8,512]{2,1,0:T(8,128)} %get-tuple-element.4.phase_in, f32[3,64,8,512]{3,2,1,0:T(8,128)} %get-tuple-element.5.flow_in), custom_call_target="tpu_custom_call" | custom-call | flops 1000000 | bytes 8388608 | tf_op jit(solution)/shard_map/pallas_call | solution.py:820

commit v3 on v2

--- a/solution.py
+++ b/solution.py
@@ -214,7 +214,9 @@
     z_inverse = np.stack([np.stack([cz, -sz], 2), np.stack([sz, cz], 2)], 1)
     z_inverse = z_inverse.reshape(2 * total_z, 2 * modes_z)
     z_rotated = np.concatenate([z_inverse[:, modes_z:], -z_inverse[:, :modes_z]], axis=1)
-    made = (x_table, y_forward, z_forward, z_inverse, z_rotated)
+    x_wide = np.stack([cos_x, -sin_x]).reshape(2, cols, kx_row * rows // cols, NX)
+    x_wide = x_wide.transpose(1, 0, 2, 3).reshape(2 * KC, NX)
+    made = (x_wide, y_forward, z_forward, z_inverse, z_rotated, x_table)
     return [jnp.asarray(t.astype(ml_dtypes.bfloat16)) for t in made]
 
 
@@ -240,17 +242,27 @@
     scale_inv = 1.0 / (NX * NY * total_z)
     made_tables = tables(cols, rows, rows_y, planes)
     f32, bf16 = jnp.float32, jnp.bfloat16
-    forward_count, derived_count, derived_lines, final_count = 8, 7, 6, 3
+    forward_count, derived_count, derived_lines, final_count = 7, 7, 6, 3
     row_count = forward_count + derived_count
     col_count = forward_count + derived_lines
     kx_col = kx_own * rows
     wide_lanes = kx_own * KY
 
+    def partner(me, d, size):
+        if size & (size - 1):
+            return lax.rem(me + d, size)
+        peer, bit = 0, 1
+        while bit < size:
+            mine = (me // bit) % 2
+            peer = peer + bit * (1 - mine if d & bit else mine)
+            bit *= 2
+        return peer
+
     def exchange(axis, size, src, dst, send, recv):
         me = lax.axis_index(axis)
 
         def copy(f, d):
-            peer = lax.rem(me + d, size)
+            peer = partner(me, d, size)
             return pltpu.make_async_remote_copy(
                 src_ref=src.at[f, peer],
                 dst_ref=dst.at[f, me],
@@ -261,7 +273,7 @@
             )
 
         def start(f):
-            for d in range(1, size):
+            for d in reversed(range(1, size)):
                 copy(f, d).start()
             dst[f, me] = src[f, me]
 
@@ -295,16 +307,16 @@
 
     def body(*refs):
         phase_in, flow_in = refs[:2]
-        table_in = refs[2:7]
-        phase_out, flow_out = refs[7:9]
+        table_in = refs[2:8]
+        phase_out, flow_out = refs[8:10]
         (
             row_src, row_dst, col_src, col_dst, thin_src, thin_dst, wide_src, wide_dst,
             fields, lines, derived, coeff, ready,
-            x_tab, yf_tab, zf_tab, zi_tab, zr_tab, xw_tab, yi_tab,
+            xw_tab, yf_tab, zf_tab, zi_tab, zr_tab, x_tab, yi_tab,
             row_send, row_recv, col_send, col_recv, thin_send, thin_recv, wide_send, wide_recv,
             load_sem, table_sem, store_sem,
-        ) = refs[9:]
-        table_refs = (x_tab, yf_tab, zf_tab, zi_tab, zr_tab)
+        ) = refs[10:]
+        table_refs = (xw_tab, yf_tab, zf_tab, zi_tab, zr_tab, x_tab)
         row_start, row_arrived, row_sent = exchange("row", rows, row_src, row_dst, row_send, row_recv)
         col_start, col_arrived, col_sent = exchange("col", cols, col_src, col_dst, col_send, col_recv)
         thin_start, thin_arrived, thin_sent = exchange(
@@ -383,34 +395,22 @@
                 row_src[h, r] = made[r * 2 * planes : (r + 1) * 2 * planes]
             row_start(h)
 
-        def wide_tables():
-            out_row = lax.broadcasted_iota(jnp.int32, (2 * KC, 2 * KC), 0)
-            in_row = lax.broadcasted_iota(jnp.int32, (2 * KC, 2 * KC), 1)
-            c = out_row // (2 * kx_col)
-            inside = out_row - c * 2 * kx_col
-            part = jnp.where(inside >= kx_col, 1, 0)
-            kx = inside - part * kx_col
-            r = kx // kx_own
-            a = c * kx_own + kx - r * kx_own
-            wanted = (2 * r + part) * kx_row + (a % 2) * pairs + a // 2
-            chosen = jnp.where(in_row == wanted, 1.0, 0.0).astype(bf16)
-            xw_tab[...] = dot(chosen, x_tab[...]).astype(bf16)
-
         def inverse_table():
             for t in range(2):
                 part = yf_tab[:, t * KY : (t + 1) * KY].astype(f32)
                 yi_tab[:, t * NY : (t + 1) * NY] = part.T.astype(bf16)
 
-        def first_x():
-            made = dot(xw_tab[...], lines[0], ((1,), (1,))).astype(bf16)
-            wide_src[0] = made.reshape(cols, 2 * kx_col, points)
-
-        def first_y():
-            wide_arrived(0)
+        def wide_x(slot, line):
+            made = dot(xw_tab[...], lines[line], ((1,), (1,))).astype(bf16)
+            wide_src[slot] = made.reshape(cols, 2 * kx_col, points)
+
+        def wide_y(slot):
+            wide_arrived(slot)
             lhs = jnp.concatenate(
                 [
                     jnp.concatenate(
-                        [wide_dst[0, c, :, z * rows_y : (z + 1) * rows_y] for c in range(cols)], axis=1
+                        [wide_dst[slot, c, :, z * rows_y : (z + 1) * rows_y] for c in range(cols)],
+                        axis=1,
                     )
                     for z in range(planes)
                 ],
@@ -423,16 +423,16 @@
             both = jnp.concatenate([real, imag], axis=1).astype(bf16)
             for k in range(kx_col):
                 r, a = k // kx_own, k % kx_own
-                thin_src[0, r, :, a * KY : (a + 1) * KY] = both[k]
-            thin_start(0)
-
-        def first_z():
-            thin_arrived(0)
-            stacked = thin_dst[0].reshape(2 * total_z, wide_lanes)
+                thin_src[slot, r, :, a * KY : (a + 1) * KY] = both[k]
+            thin_start(slot)
+
+        def wide_z(slot, f):
+            thin_arrived(slot)
+            stacked = thin_dst[slot].reshape(2 * total_z, wide_lanes)
             made = dot(zf_tab[...], stacked) * scale_inv
             for p in range(2):
                 for a in range(kx_own):
-                    coeff[0, p, a * modes_z : (a + 1) * modes_z, :] = made[
+                    coeff[f, p, a * modes_z : (a + 1) * modes_z, :] = made[
                         p * modes_z : (p + 1) * modes_z, a * KY : (a + 1) * KY
                     ]
 
@@ -568,12 +568,14 @@
                 made.append((stable * old[p] - kept - mobility * k2 * bulk_hat[p]) / below)
             put(0, made[0], made[1])
 
+        forcing_slot = (8, 6, 7)
+
         def solve_flow(get, put, wx, wy, wz, k2, mean_mode):
             viscous = 1.0 / time_step + k2 / reynolds
             largest = jnp.maximum(k2, 1.0)
             w = [wx, wy, wz]
             old = [get(1 + j) for j in range(3)]
-            added = [get(6 + j) for j in range(3)]
+            added = [get(forcing_slot[j]) for j in range(3)]
             made = [[], [], []]
             for p in range(2):
                 free = [(old[j][p] / time_step + added[j][p]) / viscous for j in range(3)]
@@ -627,29 +629,29 @@
             y_inverse(e, forward_count + e)
 
         table_copy(0).wait()
-        wide_tables()
         bring(0)
-        first_x()
+        wide_x(0, 0)
         greeted()
         wide_start(0)
+        for k in range(1, len(table_refs)):
+            table_copy(k).wait()
         for j in range(1, 4):
             bring(j)
         loop(1, 4, x_forward)
-        for k in range(1, len(table_refs)):
-            table_copy(k).wait()
         inverse_table()
         pointwise(make_bulk)
         loop(1, 3, z_forward)
-        first_y()
+        wide_y(0)
         x_forward(4)
         z_forward(3)
-        first_z()
+        wide_z(0, 0)
         spectral(derive_phase)
-        loop(0, 3, send_derived)
-        loop(1, 4, y_forward)
+        send_derived(0)
+        loop(1, 3, y_forward)
+        send_derived(1)
+        y_forward(3)
         spectral(derive_vortex)
-        loop(3, 6, send_derived)
-        z_forward(4)
+        loop(2, 6, send_derived)
 
         g0 = forward_count
         h0 = forward_count
@@ -685,7 +687,7 @@
                 potential = c * c * c - c - epsilon * epsilon * derived[3, at, :]
                 for j in which:
                     p, q = (j + 1) % 3, (j + 2) % 3
-                    lines[1 + j, at, :] = (
+                    lines[(3, 1, 2)[j], at, :] = (
                         fields[1 + p, at, :] * derived[vortex_at[q], at, :]
                         - fields[1 + q, at, :] * derived[vortex_at[p], at, :]
                         + potential * derived[gradient_at[j], at, :]
@@ -702,26 +704,29 @@
         x_forward(5)
         z_inverse(g0 + 3, h0 + 4)
         to_field(3)
+        z_forward(4)
         z_forward(5)
         z_inverse(g0 + 4, h0 + 5)
         to_field(4)
         z_inverse(g0 + 5, h0 + 6)
         to_field(5)
         pointwise(make_forcing((0,)))
-        x_forward(6)
+        wide_x(1, 3)
+        wide_start(1)
         to_field(6)
         pointwise(make_forcing((1, 2)))
-        loop(7, 9, x_forward)
-        z_forward(6)
+        loop(6, 8, x_forward)
         loop(4, 6, y_forward)
         spectral(solve_phase)
-        loop(7, 9, z_forward)
+        loop(6, 8, z_forward)
         loop(0, final_count, row_sent)
         loop(0, final_count, col_sent)
         thin_sent(0)
         wide_sent(0)
         y_inverse(0, 0)
-        loop(6, 9, y_forward)
+        wide_y(1)
+        wide_z(1, 8)
+        loop(6, 8, y_forward)
         spectral(solve_flow)
         last_z()
         def send_flow(e):
@@ -749,8 +754,8 @@
         emit(3)
         loop(0, row_count, row_sent)
         loop(0, col_count, col_sent)
-        thin_sent(0)
-        wide_sent(0)
+        loop(0, 2, thin_sent)
+        loop(0, 2, wide_sent)
         for j in range(4):
             for z in range(planes):
                 store(j, z).wait()
@@ -758,8 +763,8 @@
     sems = pltpu.SemaphoreType.DMA
     row_shape = (row_count, rows, 2 * planes, row_lanes)
     col_shape = (col_count, cols, 2 * modes_z, col_lanes)
-    thin_shape = (1, rows, 2 * planes, wide_lanes)
-    wide_shape = (1, cols, 2 * kx_col, points)
+    thin_shape = (2, rows, 2 * planes, wide_lanes)
+    wide_shape = (2, cols, 2 * kx_col, points)
     scratch = []
     for shape in (row_shape, col_shape, thin_shape, wide_shape):
         scratch += [pltpu.VMEM(shape, bf16), pltpu.VMEM(shape, bf16)]
@@ -771,7 +776,7 @@
         pltpu.VMEM((derived_lines, 2 * own, KY), bf16),
     ]
     scratch += [pltpu.VMEM(t.shape, bf16) for t in made_tables]
-    scratch += [pltpu.VMEM((2 * KC, NX), bf16), pltpu.VMEM((KY, 2 * NY), bf16)]
+    scratch += [pltpu.VMEM((KY, 2 * NY), bf16)]
     for shape, size in ((row_shape, rows), (col_shape, cols), (thin_shape, rows), (wide_shape, cols)):
         scratch += [sems((shape[0], size - 1)), sems((shape[0], size - 1))]
     scratch += [sems((4, planes)), sems((len(made_tables),)), sems((4, planes))]

time: 152 us -> 147 us (0.967)
  the two profiles are of different devices: /device:TPU:27 before, /device:TPU:0 now
where the time goes in v3:
time: 147 us
  Pallas kernels  146 us (99%)
    pallas_call x1, Pallas kernels, fast_device(): pl.pallas_call(body, in_specs=[hbm] * (2 + len(made_tables)), out_specs=[...  143 us
    pallas_call x1, Pallas kernels, fast_device(): pl.pallas_call(deliver, in_specs=[hbm, hbm], out_specs=[hbm, hbm], out_sh...  3.85 us

profile of v3, /device:TPU:0, one launch (start us, length us, event | category | flops | bytes accessed | tf_op | source)
XLA Modules:
  0.0 147.2 jit_solution(8072200219124505404)
XLA Ops:
  0.6 142.6 %shard_map.95 = (f32[64,8,512]{2,1,0:T(8,128)}, f32[3,64,8,512]{3,2,1,0:T(8,128)}) custom-call(f32[64,8,512]{2,1,0:T(8,128)} %refs_0_.1, f32[3,64,8,512]{3,2,1,0:T(8,128)} %refs_1_.1, bf16[384,512]{1,0:T(8,128)(2,1)} %constant.12.clone.refs_2_, bf16[512,768]{1,0:T(8,128)(2,1)} %constant.13.clone.refs_3_, bf16[48,64]{1,0:T(8,128)(2,1)} %constant.14.clone.refs_4_, ...), custom_call_target="tpu_custom_call" | custom-call | flops 8000000000 | bytes 8388608 | tf_op jit(solution)/shard_map/pallas_call | solution.py:788
  143.2 3.9 %shard_map.96 = (f32[64,8,512]{2,1,0:T(8,128)}, f32[3,64,8,512]{3,2,1,0:T(8,128)}) custom-call(f32[64,8,512]{2,1,0:T(8,128)} %get-tuple-element.4.phase_in, f32[3,64,8,512]{3,2,1,0:T(8,128)} %get-tuple-element.5.flow_in), custom_call_target="tpu_custom_call" | custom-call | flops 1000000 | bytes 8388608 | tf_op jit(solution)/shard_map/pallas_call | solution.py:825

commit v4 on v3

--- a/solution.py
+++ b/solution.py
@@ -651,7 +651,7 @@
         send_derived(1)
         y_forward(3)
         spectral(derive_vortex)
-        loop(2, 6, send_derived)
+        loop(2, 5, send_derived)
 
         g0 = forward_count
         h0 = forward_count
@@ -696,6 +696,7 @@
             return work
 
         phase_planes()
+        send_derived(5)
         z_inverse(g0 + 1, h0 + 2)
         loop(0, 2, to_field)
         z_inverse(g0 + 2, h0 + 3)
@@ -716,9 +717,9 @@
         to_field(6)
         pointwise(make_forcing((1, 2)))
         loop(6, 8, x_forward)
+        loop(6, 8, z_forward)
         loop(4, 6, y_forward)
         spectral(solve_phase)
-        loop(6, 8, z_forward)
         loop(0, final_count, row_sent)
         loop(0, final_count, col_sent)
         thin_sent(0)
@@ -799,7 +800,7 @@
         ),
     )(phase, velocity, *made_tables)
 
-    cuts = 4
+    cuts = 2
     part = rows_y // cuts
 
     def deliver(phase_in, flow_in, phase_out, flow_out, held, load_sem, store_sem):

time: 147 us -> 147 us (level)
  no operation moved by 1% of the time
where the time goes in v4:
time: 147 us
  Pallas kernels  146 us (99%)
    pallas_call x1, Pallas kernels, fast_device(): pl.pallas_call(body, in_specs=[hbm] * (2 + len(made_tables)), out_specs=[...  143 us
    pallas_call x1, Pallas kernels, fast_device(): pl.pallas_call(deliver, in_specs=[hbm, hbm], out_specs=[hbm, hbm], out_sh...  3.58 us

profile of v4, /device:TPU:0, one launch (start us, length us, event | category | flops | bytes accessed | tf_op | source)
XLA Modules:
  0.0 147.0 jit_solution(4818948045857231952)
XLA Ops:
  0.6 142.6 %shard_map.95 = (f32[64,8,512]{2,1,0:T(8,128)}, f32[3,64,8,512]{3,2,1,0:T(8,128)}) custom-call(f32[64,8,512]{2,1,0:T(8,128)} %refs_0_.1, f32[3,64,8,512]{3,2,1,0:T(8,128)} %refs_1_.1, bf16[384,512]{1,0:T(8,128)(2,1)} %constant.12.clone.refs_2_, bf16[512,768]{1,0:T(8,128)(2,1)} %constant.13.clone.refs_3_, bf16[48,64]{1,0:T(8,128)(2,1)} %constant.14.clone.refs_4_, ...), custom_call_target="tpu_custom_call" | custom-call | flops 8000000000 | bytes 8388608 | tf_op jit(solution)/shard_map/pallas_call | solution.py:789
  143.2 3.6 %shard_map.96 = (f32[64,8,512]{2,1,0:T(8,128)}, f32[3,64,8,512]{3,2,1,0:T(8,128)}) custom-call(f32[64,8,512]{2,1,0:T(8,128)} %get-tuple-element.4.phase_in, f32[3,64,8,512]{3,2,1,0:T(8,128)} %get-tuple-element.5.flow_in), custom_call_target="tpu_custom_call" | custom-call | flops 1000000 | bytes 8388608 | tf_op jit(solution)/shard_map/pallas_call | solution.py:826
